TPU v7x, 256 devices: a 8x8x2 block of a 8x8x16 slice. The times are simulated.
256 devices in a mesh: parts: 2 (over z), genes: 64 (over x, y), samples: 2 (over core).
Axes of the slice: x: 8, y: 8, z: 2, core: 2. Of those that a mesh axis runs over, the one named last changes fastest.
The devices are a block of a 8x8x16 slice.
Arguments:
- dosage: bfloat16 [262144, 2048], P(('parts', 'genes'), 'samples'), parts along dimension 0, may hold values from -6 to 6
- expression: bfloat16 [1024, 2048], P(('parts', 'genes'), 'samples'), parts along dimension 0, may hold values from -6 to 6
- intron_counts: bfloat16 [4096, 20480], P(('parts', 'samples', 'genes')), parts along dimension 0, may hold values from 1 to 100
- cluster_sizes: int32 [1024, 8], P('parts'), parts along dimension 0, may hold values from 1 to 12, 40 in all within a row
- valid_mask: int32 [1024, 40], P('parts'), parts along dimension 0, may hold values 0 or 1
- gene_block: int32 [1024], P('parts'), parts along dimension 0, may hold values from 0 to 511, each once
- window_start: int32 [1024], P(('parts', 'genes')), parts along dimension 0, may hold values from 0 to 1024, as said below
Outputs:
- assoc: bfloat16 [1024, 41, 2048], P(('parts', 'genes'), None, 'samples'), parts along dimension 0
There are 2 independent parts, one for each index of `parts`. A program takes and returns all parts, laid end to end along the dimension named above; each array names one. Nothing has to cross between parts.
Inputs may be any that keep to these rules, and one draw needn't show every extreme that they name: Every window_start is a multiple of 128 and at most 1024; some gene reaches 1024 in every draw. `gene_block`: a permutation of the genes. `cluster_sizes`: each row sums to 40.
All inputs are finite; a program needn't handle non-finite values.
Results may differ from a plain program's by a relative error of at most 0.0058.
Values may be sent and summed in bfloat16 or wider, within the bound.
No kernel may reach another device: no remote copies, remote signals or barrier semaphores. Data moves between devices by JAX's collectives and lax.ppermute only.
A program may use at most 64 MiB of HBM per device.

v0:
```python
import jax
import jax.numpy as jnp
from jax import lax
from jax.sharding import PartitionSpec as P

W = 2048
SLOTS = 40
SPILL = 1024
ALIGN = 128
PHEN = 41


def shifted(block, axis, distance):
    devices = range(lax.axis_size(axis))
    route = [(i - distance, i) for i in devices if i - distance in devices]
    return lax.ppermute(block, axis, route)


def together(arrays, axis):
    vector, at, finished = (jnp.concatenate([a.reshape(-1) for a in arrays]), 0, [])
    subtotal = lax.psum(vector, axis)
    for a in arrays:
        finished.append(subtotal[at : at + a.size].reshape(a.shape))
        at += a.size
    return tuple(finished)


def in_blocks(x, dim, count):
    shape = x.shape
    parts = x.reshape(*shape[:dim], count, shape[dim] // count, *shape[dim + 1 :])
    return jnp.moveaxis(parts, dim, 0)


def summed_on_arrival(x, axis, dim):
    count = lax.axis_size(axis)
    parts = lax.all_to_all(in_blocks(x, dim, count), axis, 0, 0, tiled=True)
    return jnp.sum(parts, axis=0)


def cluster_ratios(counts, cluster_sizes, valid_mask):
    cluster_ends = jnp.cumsum(cluster_sizes, axis=1, dtype=jnp.int32)
    slot_index = jnp.arange(SLOTS, dtype=jnp.int32)
    cluster_id = jnp.sum(
        (cluster_ends[:, None, :] <= slot_index[None, :, None]).astype(jnp.int32),
        axis=2,
        dtype=jnp.int32,
    )
    same_cluster = (cluster_id[:, :, None] == cluster_id[:, None, :]).astype(jnp.float32)
    live_counts = counts * valid_mask.astype(jnp.float32)[None, :, :]
    cluster_total = jnp.einsum(
        "sgj,gjk->sgk", live_counts, same_cluster, precision=lax.Precision.HIGHEST
    )
    return (live_counts / jnp.maximum(cluster_total, 1.0)).astype(jnp.bfloat16)


def tile_window(owner_block, offset, width):
    leading = owner_block.shape[:-1]
    tiles = owner_block.reshape(leading + (owner_block.shape[-1] // ALIGN, ALIGN))
    first_tile = offset // ALIGN
    piece = lax.dynamic_slice_in_dim(tiles, first_tile, width // ALIGN, len(leading))
    return piece.reshape(leading + (width,))


def window_slices(product, row_sum, row_square, starts, width):

    def window_of(owner_block, offset):
        return tile_window(owner_block, offset, width)

    cross_part = jax.vmap(window_of, in_axes=(0, 0))(product, starts)
    sum_part = jax.vmap(window_of, in_axes=(None, 0))(row_sum, starts)
    square_part = jax.vmap(window_of, in_axes=(None, 0))(row_square, starts)
    return (cross_part, sum_part, square_part)


def finish_stats(cross_part, sum_part, square_part, phen_sum, phen_square, sample_count):
    numerator = cross_part - sum_part[:, None, :] * phen_sum[:, :, None] / sample_count
    dose_var = jnp.maximum(square_part - sum_part * sum_part / sample_count, 1.0)
    pheno_var = jnp.maximum(phen_square - phen_sum * phen_sum / sample_count, 1.0)
    return (numerator * lax.rsqrt(dose_var)[:, None, :] * lax.rsqrt(pheno_var)[:, :, None]).astype(
        jnp.bfloat16
    )


def shards(dosage, expression, intron_counts, cluster_sizes, valid_mask, gene_block, window_start):
    samp_dev = dosage.shape[1]
    gene_dev = expression.shape[0]
    total_genes = gene_block.shape[0]
    next_rows = shifted(dosage[:SPILL], "genes", -1)
    dose_rows = jnp.concatenate([dosage, next_rows], axis=0)
    stored = intron_counts.reshape(intron_counts.shape[0], total_genes, SLOTS)
    counts = jnp.take(stored, gene_block, axis=1).astype(jnp.float32)
    ratios = cluster_ratios(counts, cluster_sizes, valid_mask).reshape(
        intron_counts.shape[0], total_genes * SLOTS
    )
    exchanged = lax.all_to_all(ratios, "genes", split_axis=1, concat_axis=0, tiled=True)
    intron_panel = exchanged.reshape(samp_dev, gene_dev, SLOTS)
    n_samples = lax.axis_size("samples")
    half_width = W // n_samples
    offset = lax.axis_index("samples") * half_width
    contract = (((0,), (1,)), ((), ()))
    pheno_panel = jnp.concatenate([expression.T[:, :, None], intron_panel], axis=2).reshape(
        samp_dev, gene_dev * PHEN
    )
    product = lax.dot_general(pheno_panel, dose_rows, contract, preferred_element_type=jnp.float32)
    product = product.reshape(gene_dev, PHEN, W + SPILL)
    pheno_float = pheno_panel.astype(jnp.float32)
    phen_sum = jnp.sum(pheno_float, axis=0).reshape(gene_dev, PHEN)
    phen_square = jnp.sum(pheno_float * pheno_float, axis=0).reshape(gene_dev, PHEN)
    dose_float = dose_rows.astype(jnp.float32)
    row_sum = jnp.sum(dose_float, axis=1)
    row_square = jnp.sum(dose_float * dose_float, axis=1)
    row_sum, row_square, phen_sum, phen_square = together(
        (row_sum, row_square, phen_sum, phen_square), "samples"
    )
    cross_part, sum_part, square_part = window_slices(product, row_sum, row_square, window_start, W)
    cross_sums = summed_on_arrival(cross_part, "samples", 2)
    sum_half = lax.dynamic_slice_in_dim(sum_part, offset, half_width, 1)
    square_half = lax.dynamic_slice_in_dim(square_part, offset, half_width, 1)
    sample_count = float(samp_dev * n_samples)
    return finish_stats(cross_sums, sum_half, square_half, phen_sum, phen_square, sample_count)


def solution(mesh):
    in_specs = (
        P(("parts", "genes"), "samples"),
        P(("parts", "genes"), "samples"),
        P(("parts", "samples", "genes"), None),
        P("parts", None),
        P("parts", None),
        P("parts"),
        P(("parts", "genes")),
    )
    out_specs = P(("parts", "genes"), None, "samples")
    return jax.shard_map(shards, mesh=mesh, in_specs=in_specs, out_specs=out_specs, check_vma=False)
```

profile of v0, /device:TPU:515, one launch (start us, length us, event | category | flops | bytes accessed | tf_op | source)
XLA Modules:
  0.0 155.1 jit_solution(954485686904478293)
XLA Ops:
  0.0 3.1 %slice.15 = bf16[1024,1024]{1,0:T(8,128)(2,1)} slice(bf16[2048,1024]{1,0:T(8,128)(2,1)} %param.7), slice={[0:1024], [0:1024]} | slice | bytes 4194304 | tf_op jit(solution)/shard_map/slice | solution.py:88
  3.1 13.4 %collective-permute-start = (bf16[1024,1024]{1,0:T(8,128)(2,1)}, bf16[1024,1024]{1,0:T(8,128)(2,1)}, u32[]{:S(2)}, u32[]{:S(2)}) collective-permute-start(bf16[1024,1024]{1,0:T(8,128)(2,1)} %slice.15), channel_id=1, source_target_pairs={{2,0},{4,2},{6,4},{8,6},{10,8},{12,10},{14,12},{16,14},{18,16},{20... | collective-permute-start | bytes 6291464 | tf_op jit(solution)/shard_map/ppermute | solution.py:16
  16.5 4.9 %reshape.65 = bf16[16,512,40]{2,1,0:T(8,128)(2,1)} reshape(bf16[16,20480]{1,0:T(8,128)(2,1)S(1)} %copy-done) | data formatting | bytes 1310720 | tf_op jit(solution)/shard_map/reshape | solution.py:90
  21.4 2.9 %copy.89 = bf16[16,512,40]{2,0,1:T(8,128)(2,1)S(1)} copy(bf16[16,512,40]{2,1,0:T(8,128)(2,1)} %reshape.65) | data formatting | bytes 1310720 | tf_op jit(solution)/shard_map/reshape | solution.py:90
  24.4 2.8 %gather_fusion = bf16[512,16,40]{2,1,0:T(8,128)(2,1)} fusion(bf16[16,512,40]{2,0,1:T(8,128)(2,1)S(1)} %copy.89, s32[1024]{0:T(1024)S(1)} %pad_clamp_fusion), kind=kCustom, calls=%fused_computation | custom fusion | bytes 1312768 | tf_op jit(solution)/shard_map/jit(_take)/gather | solution.py:91
  27.2 2.5 %copy.90 = bf16[512,16,40]{0,2,1:T(8,128)(2,1)S(1)} copy(bf16[512,16,40]{2,1,0:T(8,128)(2,1)} %gather_fusion) | data formatting | bytes 1310720 | tf_op jit(solution)/shard_map/jit(_take)/gather | solution.py:91
  29.9 3.7 %copy.93 = f32[16,512,40]{2,0,1:T(8,128)} copy(f32[16,512,40]{1,2,0:T(8,128)S(1)} %multiply_bitcast_fusion) | data formatting | bytes 2621440 | tf_op jit(solution)/shard_map/mul | solution.py:49
  34.0 10.0 %fusion.1 = f32[512,40,16]{1,2,0:T(8,128)} fusion(f32[16,512,40]{2,0,1:T(8,128)} %copy.93, s32[512,40]{1,0:T(8,128)S(1)} %copy.91), kind=kOutput, calls=%fused_computation.9 | convolution fusion | flops 158105600 | bytes 2703360 | tf_op jit(solution)/shard_map/sgj,gjk->sgk/dot_general | solution.py:50
  44.0 2.8 %copy.94 = f32[512,40,16]{0,1,2:T(8,128)S(1)} copy(f32[512,40,16]{1,2,0:T(8,128)} %fusion.1) | data formatting | bytes 2621440 | tf_op jit(solution)/shard_map/sgj,gjk->sgk/dot_general | solution.py:50
  47.1 1.1 copy.95
  48.2 1.4 all_to_all.15
  49.6 1.4 copy.96
  51.0 8.7 %all-to-all-start = ((bf16[16,64,320]{2,0,1:T(8,128)(2,1)}), bf16[16,64,320]{2,0,1:T(8,128)(2,1)S(1)}, u32[]{:S(2)}, u32[]{:S(2)}) async-start(bf16[16,64,320]{2,0,1:T(8,128)(2,1)} %copy.96), calls=%async_computation | async-start | bytes 1572864 | tf_op jit(solution)/shard_map/all_to_all | solution.py:95
  59.7 4.6 %constant_dynamic-update-slice_fusion.1 = bf16[3072,1024]{1,0:T(8,128)(2,1)} fusion(bf16[2048,1024]{1,0:T(8,128)(2,1)} %param.7), kind=kLoop, calls=%fused_computation.34 | loop fusion | bytes 8388608
  64.3 19.8 %all-to-all-done = bf16[16,64,320]{2,0,1:T(8,128)(2,1)S(1)} async-done(((bf16[16,64,320]{2,0,1:T(8,128)(2,1)}), bf16[16,64,320]{2,0,1:T(8,128)(2,1)S(1)}, u32[]{:S(2)}, u32[]{:S(2)}) %all-to-all-start) | async-done | bytes 655392 | tf_op jit(solution)/shard_map/all_to_all | solution.py:95
  84.0 1.8 %reshape.66 = bf16[1024,8,40]{2,1,0:T(8,128)(2,1)S(1)} reshape(bf16[64,16,320]{2,1,0:T(8,128)(2,1)S(1)} %bitcast.58) | data formatting | bytes 1310720 | tf_op jit(solution)/shard_map/reshape | solution.py:96
  85.8 2.1 %copy.97 = bf16[1024,8,40]{0,1,2:T(8,128)(2,1)S(1)} copy(bf16[1024,8,40]{2,1,0:T(8,128)(2,1)S(1)} %reshape.66) | data formatting | bytes 1310720 | tf_op jit(solution)/shard_map/reshape | solution.py:96
  89.4 3.1 %constant_dynamic-update-slice_fusion = bf16[3072,1024]{1,0:T(8,128)(2,1)} fusion(bf16[3072,1024]{1,0:T(8,128)(2,1)} %constant_dynamic-update-slice_fusion.1, bf16[1024,1024]{1,0:T(8,128)(2,1)} %collective-permute-done), kind=kLoop, calls=%fused_computation.33 | loop fusion | bytes 4194304 | tf_op jit(solution)/shard_map/concatenate | solution.py:89
  92.5 4.7 %fusion = (f32[3072]{0:T(1024)S(1)}, f32[3072]{0:T(1024)S(1)}) fusion(bf16[3072,1024]{1,0:T(8,128)(2,1)} %constant_dynamic-update-slice_fusion), kind=kLoop, calls=%fused_computation.8 | loop fusion | flops 12576768 | bytes 6316032 | tf_op jit(solution)/shard_map/reduce_sum | solution.py:111
  97.2 7.0 %psum.7 = f32[6800]{0:T(1024)S(1)} all-reduce(f32[6800]{0:T(1024)S(1)} %concatenate.19), channel_id=1, replica_groups=mesh['parts'=2,'genes'=64,'samples'=2] {'samples'}, use_global_device_ids=true, to_apply=%region_7.8 | all-reduce | flops 6800 | bytes 54400 | tf_op jit(solution)/shard_map/psum | solution.py:21
  104.3 9.6 %while.2 = (s32[]{:T(128)}, f32[24,128]{1,0:T(8,128)S(1)}, s32[8,2]{0,1:T(2,128)S(1)}, f32[8,16,128]{2,1,0:T(8,128)S(1)}, s32[]{:T(128)}) while((s32[]{:T(128)}, f32[24,128]{1,0:T(8,128)S(1)}, s32[8,2]{0,1:T(2,128)S(1)}, f32[8,16,128]{2,1,0:T(8,128)S(1)}, s32[]{:T(128)}) %tuple.36), condition=%wide.while_cond, body=%wide.while_body.sunk | while | flops 2 | bytes 16481 | solution.py:60
  104.9 0.6 bitcast_dynamic-update-slice_fusion.4
  106.1 0.6 bitcast_dynamic-update-slice_fusion.4
  107.3 0.6 bitcast_dynamic-update-slice_fusion.4
  108.5 0.6 bitcast_dynamic-update-slice_fusion.4
  109.7 0.6 bitcast_dynamic-update-slice_fusion.4
  110.9 0.6 bitcast_dynamic-update-slice_fusion.4
  112.1 0.6 bitcast_dynamic-update-slice_fusion.4
  113.3 0.6 bitcast_dynamic-update-slice_fusion.4
  113.9 9.6 %while.3 = (s32[]{:T(128)}, f32[24,128]{1,0:T(8,128)S(1)}, s32[8,2]{0,1:T(2,128)S(1)}, f32[8,16,128]{2,1,0:T(8,128)S(1)}, s32[]{:T(128)}) while((s32[]{:T(128)}, f32[24,128]{1,0:T(8,128)S(1)}, s32[8,2]{0,1:T(2,128)S(1)}, f32[8,16,128]{2,1,0:T(8,128)S(1)}, s32[]{:T(128)}) %tuple.39), condition=%wide.while_cond.1, body=%wide.while_body.1.sunk | while | flops 2 | bytes 16481 | solution.py:60
  114.5 0.6 bitcast_dynamic-update-slice_fusion.5
  115.7 0.6 bitcast_dynamic-update-slice_fusion.5
  116.9 0.6 bitcast_dynamic-update-slice_fusion.5
  118.1 0.6 bitcast_dynamic-update-slice_fusion.5
  119.3 0.6 bitcast_dynamic-update-slice_fusion.5
  120.5 0.6 bitcast_dynamic-update-slice_fusion.5
  121.7 0.6 bitcast_dynamic-update-slice_fusion.5
  122.9 0.6 bitcast_dynamic-update-slice_fusion.5
  123.6 8.7 %fusion.12 = f32[8,41,24,128]{3,1,0,2:T(8,128)} fusion(bf16[8,41,1024,1]{2,1,0,3:T(8,128)(2,1)S(1)} %reshape.127, bf16[24,128,1024,1]{2,1,3,0:T(8,128)(2,1)} %bitcast.56), kind=kOutput, calls=%fused_computation.46 | convolution fusion | flops 2063597568 | bytes 10993664 | tf_op jit(solution)/shard_map/dot_general | solution.py:104
  132.3 3.1 %gather_fusion.1 = f32[8,41,16,128]{3,1,2,0:T(8,128)S(1)} fusion(f32[8,41,24,128]{3,1,0,2:T(8,128)} %fusion.12, s32[8]{0:T(128)S(1)} %or_bitcast_fusion), kind=kCustom, calls=%fused_computation.1 | custom fusion | bytes 5374080 | tf_op jit(solution)/shard_map/vmap()/gather | solution.py:60
  135.4 2.3 %copy.100 = f32[8,41,16,128]{3,2,1,0:T(8,128)} copy(f32[8,41,16,128]{3,1,2,0:T(8,128)S(1)} %gather_fusion.1) | data formatting | bytes 5373952 | tf_op jit(solution)/shard_map/vmap()/gather | solution.py:60
  137.7 3.1 %reshape.68 = f32[8,41,2,1024]{3,2,1,0:T(2,128)S(1)} reshape(f32[8,41,16,128]{3,2,1,0:T(8,128)} %copy.100) | data formatting | bytes 5373952 | tf_op jit(solution)/shard_map/reshape;vmap()/reshape | solution.py:30
  140.8 2.3 %copy.101 = f32[2,8,41,1024]{3,1,2,0:T(8,128)} copy(f32[2,8,41,1024]{3,0,2,1:T(2,128)S(1)} %bitcast.57) | data formatting | bytes 5373952 | tf_op jit(solution)/shard_map/transpose | solution.py:31
  143.2 4.0 %all-to-all-start.1 = ((f32[2,8,41,1024]{3,1,2,0:T(8,128)}), f32[2,8,41,1024]{3,1,2,0:T(8,128)S(1)}, u32[]{:S(2)}, u32[]{:S(2)}) async-start(f32[2,8,41,1024]{3,1,2,0:T(8,128)} %copy.101), calls=%async_computation.1 | async-start | bytes 5373952 | tf_op jit(solution)/shard_map/all_to_all | solution.py:36
  147.3 2.8 %all-to-all-done.1 = f32[2,8,41,1024]{3,1,2,0:T(8,128)S(1)} async-done(((f32[2,8,41,1024]{3,1,2,0:T(8,128)}), f32[2,8,41,1024]{3,1,2,0:T(8,128)S(1)}, u32[]{:S(2)}, u32[]{:S(2)}) %all-to-all-start.1) | async-done | bytes 2687008 | tf_op jit(solution)/shard_map/all_to_all | solution.py:36
  150.2 1.4 reduce_sum.59
  151.6 2.3 %fusion.7 = bf16[8,41,1024]{2,1,0:T(8,128)(2,1)S(1)} fusion(f32[8,41,1024]{2,0,1:T(8,128)} %reduce_sum.59, f32[8,41]{1,0:T(8,128)S(1)} %maximum_rsqrt_fusion.1, f32[8,1024]{1,0:T(8,128)S(1)} %get-tuple-element.42, f32[8,41]{1,0:T(8,128)S(1)} %mul.65, f32[8,1024]{1,0:T(8,128)S(1)} %get-tuple-element.41), kind=kLoop, calls=%fused_computation.18 | loop fusion | flops 2015232 | bytes 2083392 | tf_op jit(solution)/shard_map/convert_element_type | solution.py:79
  153.9 1.2 copy.105
  (76 shorter events, 12.3 us)
Async XLA Ops:
  0.0 16.5 %copy-start.4 = (s32[512]{0:T(512)S(1)}, s32[512]{0:T(512)}, u32[]{:S(2)}) copy-start(s32[512]{0:T(512)} %param.12) | copy-start | bytes 6148
  0.0 16.5 %copy-start = (bf16[16,20480]{1,0:T(8,128)(2,1)S(1)}, bf16[16,20480]{1,0:T(8,128)(2,1)}, u32[]{:S(2)}) copy-start(bf16[16,20480]{1,0:T(8,128)(2,1)} %param.9) | copy-start | bytes 1966084
  3.1 86.3 %collective-permute-start = (bf16[1024,1024]{1,0:T(8,128)(2,1)}, bf16[1024,1024]{1,0:T(8,128)(2,1)}, u32[]{:S(2)}, u32[]{:S(2)}) collective-permute-start(bf16[1024,1024]{1,0:T(8,128)(2,1)} %slice.15), channel_id=1, source_target_pairs={{2,0},{4,2},{6,4},{8,6},{10,8},{12,10},{14,12},{16,14},{18,16},{20... | collective-permute-start | bytes 6291464 | tf_op jit(solution)/shard_map/ppermute | solution.py:16
  27.1 2.5 %copy-start.1 = (s32[512,40]{0,1:T(8,128)S(1)}, s32[512,40]{0,1:T(8,128)}, u32[]{:S(2)}) copy-start(s32[512,40]{0,1:T(8,128)} %param.11) | copy-start | bytes 245764
  29.9 3.7 %copy-start.3 = (s32[512,8]{0,1:T(8,128)S(1)}, s32[512,8]{0,1:T(8,128)}, u32[]{:S(2)}) copy-start(s32[512,8]{0,1:T(8,128)} %param.10) | copy-start | bytes 49156
  49.6 10.0 %copy-start.5 = (s32[8]{0:T(128)S(1)}, s32[8]{0:T(128)}, u32[]{:S(2)}) copy-start(s32[8]{0:T(128)} %param.13) | copy-start | bytes 100
  51.0 33.1 %all-to-all-start = ((bf16[16,64,320]{2,0,1:T(8,128)(2,1)}), bf16[16,64,320]{2,0,1:T(8,128)(2,1)S(1)}, u32[]{:S(2)}, u32[]{:S(2)}) async-start(bf16[16,64,320]{2,0,1:T(8,128)(2,1)} %copy.96), calls=%async_computation | async-start | bytes 1572864 | tf_op jit(solution)/shard_map/all_to_all | solution.py:95
  85.8 2.1 %copy-start.2 = (bf16[8,1024]{1,0:T(8,128)(2,1)S(1)}, bf16[8,1024]{1,0:T(8,128)(2,1)}, u32[]{:S(2)}) copy-start(bf16[8,1024]{1,0:T(8,128)(2,1)} %param.8) | copy-start | bytes 49156
  143.2 7.0 %all-to-all-start.1 = ((f32[2,8,41,1024]{3,1,2,0:T(8,128)}), f32[2,8,41,1024]{3,1,2,0:T(8,128)S(1)}, u32[]{:S(2)}, u32[]{:S(2)}) async-start(f32[2,8,41,1024]{3,1,2,0:T(8,128)} %copy.101), calls=%async_computation.1 | async-start | bytes 5373952 | tf_op jit(solution)/shard_map/all_to_all | solution.py:36
where the time goes:
time: 156 us; the launch traced here: 155 us
  local copies, waits for them, and re-layouts  70.6 us (45%)
  starting transfers between devices  26.1 us (17%)
  waiting for transfers between devices  22.6 us (14%)
  matrix products  18.7 us (12%)
  other arithmetic  9.51 us (6%)
  blocking collectives  6.96 us (4%)
    all_to_all x1, waiting for transfers between devices, shards(): lax.all_to_all(ratios, 'genes', split_axis=1, concat_axis=0, tiled=True)  19.8 us
    gather x48, local copies, waits for them, and re-layouts  18.8 us
    ppermute x1, starting transfers between devices, shifted(): return lax.ppermute(block, axis, route)  13.4 us
    dot_general x1, matrix products, cluster_ratios(): jnp.einsum('sgj,gjk->sgk', live_counts, same_cluster, precision=lax.Preci...  10 us
    all_to_all x1, starting transfers between devices, shards(): lax.all_to_all(ratios, 'genes', split_axis=1, concat_axis=0, tiled=True)  8.66 us
    dot_general x1, matrix products, shards(): lax.dot_general(pheno_panel, dose_rows, contract, preferred_element_type=...  8.66 us
    reshape x2, local copies, waits for them, and re-layouts, shards(): stored = intron_counts.reshape(intron_counts.shape[0], total_genes, SLOTS)  7.84 us
    psum x1, blocking collectives, together(): subtotal = lax.psum(vector, axis)  6.96 us
  transfers between devices with their start and end apart: 3, of which 2 were waited for; matrix products, arithmetic and copies ran while one was open for 28% of the time, Pallas kernels for 0%

commit v1 on v0

v1 whole, which is shorter than its diff:
```python
import functools

import jax
import jax.numpy as jnp
from jax import lax
from jax.experimental import pallas as pl
from jax.experimental.pallas import tpu as pltpu
from jax.sharding import PartitionSpec as P


W = 2048
SLOTS = 40
CLUST = 8
SPILL = 1024
HALF = 1024
GENE_DEV = 8
GROUP = 4
LANES = 128
WIDE = 384
RATIOS = SLOTS * GROUP
ROWS = RATIOS + 8
ONES = RATIOS + GROUP
F32 = jnp.float32
BF16 = jnp.bfloat16

VMEM = pl.BlockSpec(memory_space=pltpu.VMEM)
SMEM = pl.BlockSpec(memory_space=pltpu.SMEM)
HBM = pl.BlockSpec(memory_space=pltpu.HBM)


def params(mib):
    return pltpu.CompilerParams(vmem_limit_bytes=mib * 1024 * 1024)


def cost(flops, nbytes):
    return pl.CostEstimate(flops=flops, bytes_accessed=nbytes, transcendentals=0)


def gather_kernel(block_hbm, counts_hbm, out_ref, block_ref, counts_ref, sems):
    blocks_in = pltpu.make_async_copy(block_hbm, block_ref, sems.at[0])
    counts_in = pltpu.make_async_copy(counts_hbm, counts_ref, sems.at[1])
    blocks_in.start()
    counts_in.start()
    samples = counts_ref.shape[0]
    owners = out_ref.shape[0]
    last = counts_ref.shape[1] // LANES - 1
    lane = lax.broadcasted_iota(jnp.int32, (samples, LANES), 1)
    low = lax.broadcasted_iota(jnp.int32, (samples // 2, LANES), 1) < 64
    out_ref[0, 0:40, :] = jnp.zeros((40, LANES), BF16)
    blocks_in.wait()
    counts_in.wait()

    def column(index):
        start = pl.multiple_of(index * LANES, LANES)
        return counts_ref[:, pl.ds(start, LANES)].astype(F32)

    def owner(o, carry):
        g = []
        for i in range(GENE_DEV):
            first = block_ref[o * GENE_DEV + i] * SLOTS
            tile = lax.shift_right_logical(first, 7)
            inside = first & (LANES - 1)
            both = jnp.where(
                lane >= inside, column(tile), column(jnp.minimum(tile + 1, last))
            )
            g.append(pltpu.roll(both, (SLOTS * i - inside) & (LANES - 1), 1))
        a = jnp.where(lane < 40, g[0], jnp.where(lane < 80, g[1], jnp.where(lane < 120, g[2], g[3])))
        b = jnp.where(lane < 32, g[3], jnp.where(lane < 72, g[4], jnp.where(lane < 112, g[5], g[6])))
        c = jnp.where(lane < 24, g[6], g[7])
        packed = jnp.where(low, c[: samples // 2], pltpu.roll(c[samples // 2 :], 64, 1))
        after = jnp.minimum(o + 1, owners - 1)
        for at, row in ((after, 0), (o, 40)):
            out_ref[at, row : row + 16, :] = a.astype(BF16)
            out_ref[at, row + 16 : row + 32, :] = b.astype(BF16)
            out_ref[at, row + 32 : row + 40, :] = packed.astype(BF16)
        return carry

    owner(owners - 1, 0)
    lax.fori_loop(0, owners - 1, owner, 0, unroll=9)


def gather_blocks(gene_block, counts, owners):
    return pl.pallas_call(
        gather_kernel,
        out_shape=jax.ShapeDtypeStruct((owners, 80, LANES), BF16),
        in_specs=[HBM, HBM],
        out_specs=VMEM,
        scratch_shapes=[
            pltpu.SMEM(gene_block.shape, jnp.int32),
            pltpu.VMEM(counts.shape, BF16),
            pltpu.SemaphoreType.DMA((2,)),
        ],
        compiler_params=params(8),
        cost_estimate=cost(10_000_000, 1),
        name="gather_blocks",
    )(gene_block, counts)


def panel_kernel(behind, recv_ref, expr_ref, sizes_ref, valid_ref, keep_ref, give_ref):
    me = jnp.maximum(lax.axis_index("genes") - behind, 0)
    first_core = lax.axis_index("samples") == 0
    first = me * GENE_DEV
    start = pl.multiple_of(first // LANES * LANES, LANES)
    back = (LANES - first % LANES) & (LANES - 1)
    sizes = pltpu.roll(sizes_ref[:, pl.ds(start, LANES)].astype(F32), back, 1)
    valid = pltpu.roll(valid_ref[:, pl.ds(start, LANES)].astype(F32), back, 1)
    ends, running = [], jnp.zeros((1, LANES), F32)
    for c in range(CLUST):
        running = running + sizes[c : c + 1, :]
        ends.append(running)
    ends = jnp.concatenate(ends, axis=0)

    x = lax.broadcasted_iota(jnp.int32, (LANES, WIDE), 1)
    i = lax.broadcasted_iota(jnp.int32, (LANES, WIDE), 0)
    spread = jnp.where((x >= SLOTS * i) & (x < SLOTS * i + SLOTS) & (i < GENE_DEV), 1.0, 0.0)
    spread = spread.astype(BF16)

    def slots_of(rows):
        x = lax.broadcasted_iota(jnp.int32, (rows, WIDE), 1)
        base = jnp.zeros((rows, WIDE), jnp.int32)
        for gene in range(1, GENE_DEV + 1):
            base = jnp.where(x >= SLOTS * gene, SLOTS * gene, base)
        return base, x - base

    ends_at = jnp.dot(ends.astype(BF16), spread, preferred_element_type=F32)
    base, slot = slots_of(CLUST)
    slot = slot.astype(F32)
    low = jnp.max(jnp.where(ends_at <= slot, ends_at, 0.0), axis=0, keepdims=True)
    high = jnp.min(jnp.where(ends_at > slot, ends_at, float(SLOTS)), axis=0, keepdims=True)
    base = base[0:1, :].astype(F32)
    valid_at = jnp.dot(valid.astype(BF16), spread, preferred_element_type=F32)
    _, slot40 = slots_of(SLOTS)
    row40 = lax.broadcasted_iota(jnp.int32, (SLOTS, WIDE), 0)
    live = jnp.sum(jnp.where(slot40 == row40, valid_at, 0.0), axis=0, keepdims=True)

    k = lax.broadcasted_iota(jnp.int32, (WIDE, WIDE), 0).astype(F32)
    inside = (k >= base + low) & (k < base + high)
    same = jnp.where(inside & (k < float(SLOTS * GENE_DEV)), 1.0, 0.0).astype(BF16)

    per = LANES // 16
    for t in range(recv_ref.shape[0] // per):
        owned = 40 * (1 - behind)
        piece = recv_ref[t * per : (t + 1) * per, owned : owned + 40, :].astype(F32)
        a = piece[:, 0:16, :].reshape(LANES, LANES)
        b = piece[:, 16:32, :].reshape(LANES, LANES)
        c = piece[:, 32:40, :]
        swapped = pltpu.roll(c, 64, 2)
        c = jnp.concatenate([c, swapped], axis=1).reshape(LANES, LANES)
        counts = jnp.concatenate([a, b, c], axis=1) * live
        total = jnp.dot(counts.astype(BF16), same, preferred_element_type=F32)
        ratio = counts / jnp.maximum(total, 1.0)
        lanes = slice(t * LANES, (t + 1) * LANES)
        turned = jnp.transpose(ratio)
        low_half, high_half = turned[0:RATIOS], turned[RATIOS : 2 * RATIOS]
        keep_ref[0:RATIOS, lanes] = jnp.where(first_core, low_half, high_half).astype(BF16)
        give_ref[0:RATIOS, lanes] = jnp.where(first_core, high_half, low_half).astype(BF16)
    expr = expr_ref[...].astype(F32)
    row = lax.broadcasted_iota(jnp.int32, expr.shape, 0)
    low_half = jnp.where(row < GROUP, expr, 1.0)
    high_half = jnp.where(row < GROUP, pltpu.roll(expr, GROUP, 0), 1.0)
    keep_ref[RATIOS:ROWS, :] = jnp.where(first_core, low_half, high_half).astype(BF16)
    give_ref[RATIOS:ROWS, :] = jnp.where(first_core, high_half, low_half).astype(BF16)


def make_panel(recv, expression, sizes, valid, behind):
    half = jax.ShapeDtypeStruct((ROWS, expression.shape[1]), BF16)
    return pl.pallas_call(
        functools.partial(panel_kernel, behind),
        out_shape=(half, half),
        in_specs=[VMEM] * 4,
        out_specs=(VMEM, VMEM),
        compiler_params=params(16),
        cost_estimate=cost(400_000_000, 1_400_000),
        name="make_panel",
    )(recv, expression, sizes, valid)


NT = (((1,), (1,)), ((), ()))


def row_sums(panels):
    rows = panels[0].shape[0]
    one, two = jnp.zeros((rows, LANES), F32), jnp.zeros((rows, LANES), F32)
    for panel in panels:
        for t in range(panel.shape[1] // LANES):
            p = panel[:, t * LANES : (t + 1) * LANES].astype(F32)
            one, two = one + p, two + p * p
    return jnp.sum(one, axis=1, keepdims=True), jnp.sum(two, axis=1, keepdims=True)


def square_sums(doses):
    block = doses[0].shape[0]
    folded = jnp.zeros((block, LANES), F32)
    for dose in doses:
        for t in range(dose.shape[1] // LANES):
            d = dose[:, t * LANES : (t + 1) * LANES].astype(F32)
            folded = folded + d * d
    return jnp.sum(jnp.transpose(folded), axis=0, keepdims=True)


BLOCK = 256


def panel_stats(count, keep_ref, got_ref):
    sy, syy = row_sums((keep_ref, got_ref))
    return sy / count, lax.rsqrt(jnp.maximum(syy - sy * sy / count, 1.0))


def correlations(count, keep_ref, got_ref, dose, other, stats):
    cross = lax.dot_general(keep_ref[...], dose[...], NT, preferred_element_type=F32)
    cross = cross + lax.dot_general(got_ref[...], other[...], NT, preferred_element_type=F32)
    sx = cross[ONES : ONES + 1]
    sxx = square_sums((dose, other))
    dose_scale = lax.rsqrt(jnp.maximum(sxx - sx * sx / count, 1.0))
    mean, scale = stats
    return (cross - sx * mean) * dose_scale * scale


def streamed(blocks, dose_hbm, other_hbm, doses, sems, body):
    copies = []
    for i in range(blocks):
        rows = pl.ds(i * BLOCK, BLOCK)
        for side, source in enumerate((dose_hbm, other_hbm)):
            copy = pltpu.make_async_copy(source.at[rows], doses.at[side, i], sems.at[side, i])
            copy.start()
            copies.append(copy)
    for i in range(blocks):
        copies[2 * i].wait()
        copies[2 * i + 1].wait()
        body(i, doses.at[0, i], doses.at[1, i])


def dose_scratch(blocks, samples):
    return [
        pltpu.VMEM((2, blocks, BLOCK, samples), BF16),
        pltpu.SemaphoreType.DMA((2, blocks)),
    ]


def own_product(window_start, keep, got, dosage, other, count):
    blocks = dosage.shape[0] // BLOCK
    side = jax.ShapeDtypeStruct((ROWS, HALF), BF16)

    def kernel(
        start_ref, keep_ref, got_ref, dose_hbm, other_hbm, mine_ref, theirs_ref, doses, sems, wide
    ):
        core = lax.axis_index("samples")
        stats = []

        def body(i, dose, other):
            if i == 0:
                stats.append(panel_stats(count, keep_ref, got_ref))
            lanes = slice(i * BLOCK, (i + 1) * BLOCK)
            wide[:, lanes] = correlations(count, keep_ref, got_ref, dose, other, stats[0])

        streamed(blocks, dose_hbm, other_hbm, doses, sems, body)
        wide[:, W : W + SPILL] = jnp.zeros((ROWS, SPILL), F32)
        for ref, side in ((theirs_ref, 1 - core), (mine_ref, core)):
            last = []
            for j in range(GROUP):
                begin = start_ref[GROUP * core + j] + side * HALF
                window = pl.ds(pl.multiple_of(begin, LANES), HALF)
                rows = slice(SLOTS * j, SLOTS * j + SLOTS)
                ref[rows, :] = wide[rows, window].astype(BF16)
                last.append(wide[RATIOS + j : RATIOS + j + 1, window])
            last = jnp.concatenate(last + last, axis=0)
            ref[RATIOS:ROWS, :] = last.astype(BF16)

    return pl.pallas_call(
        kernel,
        out_shape=(side, side),
        in_specs=[SMEM, VMEM, VMEM, HBM, HBM],
        out_specs=(VMEM, VMEM),
        scratch_shapes=dose_scratch(blocks, dosage.shape[1])
        + [pltpu.VMEM((ROWS, W + SPILL), F32)],
        compiler_params=params(24),
        cost_estimate=cost(1_500_000_000, 1),
        name="own_product",
    )(window_start, keep, got, dosage, other)


def spill_product(keep, got, dosage, other, count):
    blocks = SPILL // BLOCK

    def kernel(keep_ref, got_ref, dose_hbm, other_hbm, out_ref, doses, sems):
        stats = []

        def body(i, dose, other):
            if i == 0:
                stats.append(panel_stats(count, keep_ref, got_ref))
            lanes = slice(i * BLOCK, (i + 1) * BLOCK)
            value = correlations(count, keep_ref, got_ref, dose, other, stats[0])
            out_ref[:, lanes] = value.astype(BF16)

        streamed(blocks, dose_hbm, other_hbm, doses, sems, body)

    return pl.pallas_call(
        kernel,
        out_shape=jax.ShapeDtypeStruct((ROWS, SPILL), BF16),
        in_specs=[VMEM, VMEM, HBM, HBM],
        out_specs=VMEM,
        scratch_shapes=dose_scratch(blocks, dosage.shape[1]),
        compiler_params=params(16),
        cost_estimate=cost(700_000_000, 1),
        name="spill_product",
    )(keep, got, dosage, other)


def merge_kernel(start_ref, mine_ref, other_ref, back0, back1, out_ref, wide, rows48):
    core = lax.axis_index("samples")
    back = (back0, back1)
    for c in range(2):
        wide[c, :, SPILL : 2 * SPILL] = back[c][...].astype(F32)
    for own_ref, c in ((mine_ref, core), (other_ref, 1 - core)):
        every = own_ref[...].astype(F32)
        for j in range(GROUP):
            begin = start_ref[GROUP * c + j]
            window = pl.ds(pl.multiple_of(begin, LANES), HALF)
            edge = jnp.where(core == 1, HALF - begin, HALF)
            at = 48 * (GROUP * c + j)
            for rows, to in (
                (slice(SLOTS * j, SLOTS * j + SLOTS), pl.ds(pl.multiple_of(at, 8), SLOTS)),
                (slice(RATIOS + j, RATIOS + j + 1), pl.ds(at + SLOTS, 1)),
            ):
                own = every[rows, :]
                lane = lax.broadcasted_iota(jnp.int32, own.shape, 1)
                value = jnp.where(lane >= edge, wide[c, rows, window], own)
                for t in range(HALF // LANES):
                    rows48[t, to, :] = value[:, t * LANES : (t + 1) * LANES]
    for p in range(SLOTS + 1):
        row = SLOTS if p == 0 else p - 1
        for t in range(HALF // LANES):
            genes = rows48[t, pl.ds(row, GENE_DEV, stride=48), :]
            out_ref[p, :, t * LANES : (t + 1) * LANES] = genes.astype(BF16)


def merge(window_start, mine, other, back):
    return pl.pallas_call(
        merge_kernel,
        out_shape=jax.ShapeDtypeStruct((SLOTS + 1, GENE_DEV, HALF), BF16),
        in_specs=[SMEM] + [VMEM] * 4,
        out_specs=VMEM,
        scratch_shapes=[
            pltpu.VMEM((2, ROWS, 2 * SPILL), F32),
            pltpu.VMEM((HALF // LANES, 48 * GENE_DEV, LANES), F32),
        ],
        compiler_params=params(24),
        cost_estimate=cost(2_000_000, 3_500_000),
        name="merge_windows",
    )(window_start, mine, other, *back)


def shards(dosage, expression, intron_counts, cluster_sizes, valid_mask, gene_block, window_start):
    owners = lax.axis_size("genes")
    cores = lax.axis_size("samples")
    count = float(dosage.shape[1] * cores)
    onward = [(i, i + 1) for i in range(owners - 1)]
    swap = [(i, cores - 1 - i) for i in range(cores)]
    last = cores - 1
    home = [
        [((i + 1) * cores + c, i * cores + last) for i in range(owners - 1)] for c in range(cores)
    ]
    sizes, valid = cluster_sizes.T, valid_mask.T

    def exchanged(x):
        return lax.ppermute(x, "samples", swap)

    other_dose = exchanged(dosage)
    blocks = gather_blocks(gene_block, intron_counts, owners)
    prev_expression = lax.ppermute(expression, "genes", onward)
    recv = lax.all_to_all(blocks, "genes", 0, 0, tiled=True)

    keep, give = make_panel(recv, prev_expression, sizes, valid, 1)
    got = exchanged(give)
    piece = spill_product(keep, got, dosage, other_dose, count)
    back = []
    for c in range(cores):
        back.append(lax.ppermute(piece, ("genes", "samples"), home[c]))

    keep, give = make_panel(recv, expression, sizes, valid, 0)
    got = exchanged(give)
    mine, theirs = own_product(window_start, keep, got, dosage, other_dose, count)
    other = exchanged(theirs)
    out = merge(window_start, mine, other, back)
    return jnp.transpose(out, (1, 0, 2))


def solution(mesh):
    in_specs = (
        P(("parts", "genes"), "samples"),
        P(("parts", "genes"), "samples"),
        P(("parts", "samples", "genes"), None),
        P("parts", None),
        P("parts", None),
        P("parts"),
        P(("parts", "genes")),
    )
    out_specs = P(("parts", "genes"), None, "samples")
    return jax.shard_map(shards, mesh=mesh, in_specs=in_specs, out_specs=out_specs, check_vma=False)
```

time: 156 us -> 103 us (0.66)
  local copies, waits for them, and re-layouts: 70.6 us -> 2.09 us
  blocking collectives: 6.96 us -> 56.2 us
  Pallas kernels: 0 us -> 19.8 us
  matrix products: 18.7 us -> 0 us
  starting transfers between devices: 26.1 us -> 11.3 us
  waiting for transfers between devices: 22.6 us -> 12.2 us
  other arithmetic: 9.51 us -> 0 us
    all_to_all x0 -> x1, blocking collectives: none -> 56.2 us  [shards(): recv = lax.all_to_all(blocks, 'genes', 0, 0, tiled=True)]
    gather x52 -> x0, local copies, waits for them, and re-layouts: 29.5 us -> none
    all_to_all x2 -> x0, waiting for transfers between devices: 22.6 us -> none  [the longest x1 19.8 us: shards(): lax.all_to_all(ratios, 'genes', split_axis=1, concat_axis=0, tiled=True)]
    pallas_call x0 -> x6, Pallas kernels: none -> 19.8 us  [the longest x1 8.04 us: own_product(): pl.pallas_call(kernel, out_shape=(side, side), in_specs=[SMEM, VMEM, VMEM...]
    dot_general x2 -> x0, matrix products: 18.7 us -> none  [the longest x1 10 us: cluster_ratios(): jnp.einsum('sgj,gjk->sgk', live_counts, same_cluster, precision=lax.Preci...]
    reshape x9 -> x0, local copies, waits for them, and re-layouts: 15.1 us -> none  [the longest x2 7.84 us: shards(): stored = intron_counts.reshape(intron_counts.shape[0], total_genes, SLOTS)]
    all_to_all x2 -> x0, starting transfers between devices: 12.7 us -> none  [the longest x1 8.66 us: shards(): lax.all_to_all(ratios, 'genes', split_axis=1, concat_axis=0, tiled=True)]
    ppermute x1 -> x7, waiting for transfers between devices: 0.01 us -> 12.2 us  [the longest x2 8.43 us: shards(): back.append(lax.ppermute(piece, ('genes', 'samples'), home[c]))]
  transfers between devices with their start and end apart: 3 -> 7, of which waited for: 2 -> 3; matrix products, arithmetic and copies ran while one was open for 28% -> 0% of each run, Pallas kernels for 0% -> 17%
where the time goes in v1:
time: 103 us; the launch traced here: 102 us
  blocking collectives  56.2 us (55%)
  Pallas kernels  19.8 us (19%)
  waiting for transfers between devices  12.2 us (12%)
  starting transfers between devices  11.3 us (11%)
  local copies, waits for them, and re-layouts  2.09 us (2%)
    all_to_all x1, blocking collectives, shards(): recv = lax.all_to_all(blocks, 'genes', 0, 0, tiled=True)  56.2 us
    ppermute x2, waiting for transfers between devices, shards(): back.append(lax.ppermute(piece, ('genes', 'samples'), home[c]))  8.43 us
    pallas_call x1, Pallas kernels, own_product(): pl.pallas_call(kernel, out_shape=(side, side), in_specs=[SMEM, VMEM, VMEM...  8.04 us
    ppermute x4, starting transfers between devices, exchanged(): return lax.ppermute(x, 'samples', swap)  5.25 us
    ppermute x1, waiting for transfers between devices, shards(): prev_expression = lax.ppermute(expression, 'genes', onward)  3.79 us
    pallas_call x1, Pallas kernels, spill_product(): pl.pallas_call(kernel, out_shape=jax.ShapeDtypeStruct((ROWS, SPILL), BF16...  3.75 us
    pallas_call x1, Pallas kernels, gather_blocks(): pl.pallas_call(gather_kernel, out_shape=jax.ShapeDtypeStruct((owners, 80,...  3.73 us
    ppermute x2, starting transfers between devices, shards(): back.append(lax.ppermute(piece, ('genes', 'samples'), home[c]))  3.26 us
  transfers between devices with their start and end apart: 7, of which 3 were waited for; matrix products, arithmetic and copies ran while one was open for 0% of the time, Pallas kernels for 17%

profile of v1, /device:TPU:515, one launch (start us, length us, event | category | flops | bytes accessed | tf_op | source)
XLA Modules:
  0.0 101.7 jit_solution(13421524976530796614)
XLA Ops:
  0.0 0.0 copy-start
  0.0 0.6 collective-permute-start.1
  0.6 0.0 copy-start.1
  0.6 1.4 %copy-done.1 = bf16[16,20480]{1,0:T(8,128)(2,1)S(1)} copy-done((bf16[16,20480]{1,0:T(8,128)(2,1)S(1)}, bf16[16,20480]{1,0:T(8,128)(2,1)}, u32[]{:S(2)}) %copy-start.1) | copy-done | bytes 655384
  2.0 0.0 copy-start.2
  2.0 0.7 copy-done.2
  2.7 0.0 copy-start.4
  2.7 0.0 copy-start.5
  2.7 0.0 copy-start.6
  2.7 0.0 copy-start.3
  2.7 3.7 %gather_blocks.1 = bf16[64,80,128]{2,1,0:T(8,128)(2,1)S(1)} custom-call(s32[512]{0:T(512)S(1)} %copy-done.2, bf16[16,20480]{1,0:T(8,128)(2,1)S(1)} %copy-done.1), custom_call_target="tpu_custom_call" | custom-call | flops 10000000 | bytes 1 | tf_op jit(solution)/shard_map/gather_blocks/pallas_call | solution.py:83
  6.4 56.2 %all_to_all.5.recv_ref = bf16[64,80,128]{2,1,0:T(8,128)(2,1)S(1)} all-to-all(bf16[64,80,128]{2,1,0:T(8,128)(2,1)S(1)} %gather_blocks.1), channel_id=1, replica_groups=mesh['parts'=2,'genes'=64,'samples'=2] {'genes'}, dimensions={0} | all-to-all | bytes 2621440 | tf_op jit(solution)/shard_map/all_to_all | solution.py:371
  62.7 0.0 copy-done.4
  62.7 0.0 copy-done.5
  62.7 0.0 copy-done.6
  62.7 1.1 %make_panel.2 = (bf16[168,1024]{1,0:T(8,128)(2,1)S(1)}, bf16[168,1024]{1,0:T(8,128)(2,1)S(1)}) custom-call(bf16[64,80,128]{2,1,0:T(8,128)(2,1)S(1)} %all_to_all.5.recv_ref, bf16[8,1024]{1,0:T(8,128)(2,1)S(1)} %copy-done.5, s32[8,512]{1,0:T(8,128)S(1)} %bitcast.5, s32[40,512]{1,0:T(8,128)S(1)} %bitcast.3), custom_call_target="tpu_custom_call" | custom-call | flops 400000000 | bytes 1400000 | tf_op jit(solution)/shard_map/make_panel/pallas_call | solution.py:167
  63.8 3.0 %collective-permute-start = (bf16[168,1024]{1,0:T(8,128)(2,1)S(1)}, bf16[168,1024]{1,0:T(8,128)(2,1)S(1)}, u32[]{:S(2)}, u32[]{:S(2)}) collective-permute-start(bf16[168,1024]{1,0:T(8,128)(2,1)S(1)} %get-tuple-element.12), channel_id=1, source_target_pairs={{0,1},{1,0},{2,3},{3,2},{4,5},{5,4},{6,7},{7,6},{8,9},{9,8},{10,11... | collective-permute-start | bytes 1032200 | tf_op jit(solution)/shard_map/ppermute | solution.py:366
  66.7 2.8 %collective-permute-start.3 = (bf16[8,1024]{1,0:T(8,128)(2,1)S(1)}, bf16[8,1024]{1,0:T(8,128)(2,1)S(1)}, u32[]{:S(2)}, u32[]{:S(2)}) collective-permute-start(bf16[8,1024]{1,0:T(8,128)(2,1)S(1)} %copy-done.5), channel_id=1, source_target_pairs={{0,2},{2,4},{4,6},{6,8},{8,10},{10,12},{12,14},{14,16},{16,18},{18... | collective-permute-start | bytes 49160 | tf_op jit(solution)/shard_map/ppermute | solution.py:370
  69.6 3.8 %collective-permute-done.3.expr_ref = bf16[8,1024]{1,0:T(8,128)(2,1)S(1)} collective-permute-done((bf16[8,1024]{1,0:T(8,128)(2,1)S(1)}, bf16[8,1024]{1,0:T(8,128)(2,1)S(1)}, u32[]{:S(2)}, u32[]{:S(2)}) %collective-permute-start.3) | collective-permute-done | bytes 16416 | tf_op jit(solution)/shard_map/ppermute | solution.py:370
  73.3 1.1 %make_panel.3 = (bf16[168,1024]{1,0:T(8,128)(2,1)S(1)}, bf16[168,1024]{1,0:T(8,128)(2,1)S(1)}) custom-call(bf16[64,80,128]{2,1,0:T(8,128)(2,1)S(1)} %all_to_all.5.recv_ref, bf16[8,1024]{1,0:T(8,128)(2,1)S(1)} %collective-permute-done.3.expr_ref, s32[8,512]{1,0:T(8,128)S(1)} %bitcast.6, s32[40,512]{1,0:T(8,128)S(1)} %bitcast.4), custom_call_target="tpu_custom_call" | custom-call | flops 400000000 | bytes 1400000 | tf_op jit(solution)/shard_map/make_panel/pallas_call | solution.py:167
  74.4 1.3 %collective-permute-start.4 = (bf16[168,1024]{1,0:T(8,128)(2,1)S(1)}, bf16[168,1024]{1,0:T(8,128)(2,1)S(1)}, u32[]{:S(2)}, u32[]{:S(2)}) collective-permute-start(bf16[168,1024]{1,0:T(8,128)(2,1)S(1)} %get-tuple-element.16), channel_id=1, source_target_pairs={{0,1},{1,0},{2,3},{3,2},{4,5},{5,4},{6,7},{7,6},{8,9},{9,8},{10,11... | collective-permute-start | bytes 1032200 | tf_op jit(solution)/shard_map/ppermute | solution.py:366
  75.7 0.0 collective-permute-done.got_ref
  75.7 0.0 collective-permute-done.1.other_hbm
  75.7 0.0 copy-done
  75.7 0.0 copy-done.3
  75.7 8.0 %own_product.1 = (bf16[168,1024]{1,0:T(8,128)(2,1)S(1)}, bf16[168,1024]{1,0:T(8,128)(2,1)S(1)}) custom-call(s32[8]{0:T(128)S(1)} %copy-done.3, bf16[168,1024]{1,0:T(8,128)(2,1)S(1)} %get-tuple-element.11.keep_ref, bf16[168,1024]{1,0:T(8,128)(2,1)S(1)} %collective-permute-done.got_ref, bf16[2048,1024]{1,0:T(8,128)(2,1)S(1)} %copy-done, ...), custom_call_target="tpu_custom_call" | custom-call | flops 1500000000 | bytes 1 | tf_op jit(solution)/shard_map/own_product/pallas_call | solution.py:269
  83.8 0.4 collective-permute-start.2
  84.1 0.0 collective-permute-done.4.got_ref
  84.2 3.7 %spill_product.1 = bf16[168,1024]{1,0:T(8,128)(2,1)S(1)} custom-call(bf16[168,1024]{1,0:T(8,128)(2,1)S(1)} %get-tuple-element.15.keep_ref, bf16[168,1024]{1,0:T(8,128)(2,1)S(1)} %collective-permute-done.4.got_ref, bf16[2048,1024]{1,0:T(8,128)(2,1)S(1)} %copy-done, bf16[2048,1024]{1,0:T(8,128)(2,1)S(1)} %collective-permute-done.1.other_hbm), custom_call_target="tpu_custom_call" | custom-call | flops 700000000 | bytes 1 | tf_op jit(solution)/shard_map/spill_product/pallas_call | solution.py:297
  87.9 2.0 %collective-permute-start.6 = (bf16[168,1024]{1,0:T(8,128)(2,1)S(1)}, bf16[168,1024]{1,0:T(8,128)(2,1)S(1)}, u32[]{:S(2)}, u32[]{:S(2)}) collective-permute-start(bf16[168,1024]{1,0:T(8,128)(2,1)S(1)} %spill_product.1), channel_id=1, source_target_pairs={{3,1},{5,3},{7,5},{9,7},{11,9},{13,11},{15,13},{17,15},{19,17},{21... | collective-permute-start | bytes 1032200 | tf_op jit(solution)/shard_map/ppermute | solution.py:378
  89.9 1.3 %collective-permute-start.5 = (bf16[168,1024]{1,0:T(8,128)(2,1)S(1)}, bf16[168,1024]{1,0:T(8,128)(2,1)S(1)}, u32[]{:S(2)}, u32[]{:S(2)}) collective-permute-start(bf16[168,1024]{1,0:T(8,128)(2,1)S(1)} %spill_product.1), channel_id=1, source_target_pairs={{2,1},{4,3},{6,5},{8,7},{10,9},{12,11},{14,13},{16,15},{18,17},{20... | collective-permute-start | bytes 1032200 | tf_op jit(solution)/shard_map/ppermute | solution.py:378
  91.2 0.0 collective-permute-done.2.other_ref
  91.2 5.9 %collective-permute-done.6.back1 = bf16[168,1024]{1,0:T(8,128)(2,1)S(1)} collective-permute-done((bf16[168,1024]{1,0:T(8,128)(2,1)S(1)}, bf16[168,1024]{1,0:T(8,128)(2,1)S(1)}, u32[]{:S(2)}, u32[]{:S(2)}) %collective-permute-start.6) | collective-permute-done | bytes 344096 | tf_op jit(solution)/shard_map/ppermute | solution.py:378
  97.1 2.5 %collective-permute-done.5.back0 = bf16[168,1024]{1,0:T(8,128)(2,1)S(1)} collective-permute-done((bf16[168,1024]{1,0:T(8,128)(2,1)S(1)}, bf16[168,1024]{1,0:T(8,128)(2,1)S(1)}, u32[]{:S(2)}, u32[]{:S(2)}) %collective-permute-start.5) | collective-permute-done | bytes 344096 | tf_op jit(solution)/shard_map/ppermute | solution.py:378
  99.6 2.1 %merge_windows.1 = bf16[41,8,1024]{2,1,0:T(8,128)(2,1)} custom-call(s32[8]{0:T(128)S(1)} %copy-done.3, bf16[168,1024]{1,0:T(8,128)(2,1)S(1)} %get-tuple-element.13.mine_ref, bf16[168,1024]{1,0:T(8,128)(2,1)S(1)} %collective-permute-done.2.other_ref, bf16[168,1024]{1,0:T(8,128)(2,1)S(1)} %collective-permute-done.5.back0, ...), custom_call_target="tpu_custom_call" | custom-call | flops 2000000 | bytes 3500000 | tf_op jit(solution)/shard_map/merge_windows/pallas_call | solution.py:338
Async XLA Ops:
  0.0 75.7 %copy-start = (bf16[2048,1024]{1,0:T(8,128)(2,1)S(1)}, bf16[2048,1024]{1,0:T(8,128)(2,1)}, u32[]{:S(2)}) copy-start(bf16[2048,1024]{1,0:T(8,128)(2,1)} %dose_hbm.3) | copy-start | bytes 12582916
  0.0 75.7 %collective-permute-start.1 = (bf16[2048,1024]{1,0:T(8,128)(2,1)}, bf16[2048,1024]{1,0:T(8,128)(2,1)S(1)}, u32[]{:S(2)}, u32[]{:S(2)}) collective-permute-start(bf16[2048,1024]{1,0:T(8,128)(2,1)} %dose_hbm.3), channel_id=1, source_target_pairs={{0,1},{1,0},{2,3},{3,2},{4,5},{5,4},{6,7},{7,6},{8,9},{9,8},{10,11... | collective-permute-start | bytes 12582920 | tf_op jit(solution)/shard_map/ppermute | solution.py:366
  0.6 1.4 %copy-start.1 = (bf16[16,20480]{1,0:T(8,128)(2,1)S(1)}, bf16[16,20480]{1,0:T(8,128)(2,1)}, u32[]{:S(2)}) copy-start(bf16[16,20480]{1,0:T(8,128)(2,1)} %counts_hbm.1) | copy-start | bytes 1966084
  2.0 0.7 copy-start.2
  2.7 60.0 %copy-start.4 = (s32[512,40]{0,1:T(8,128)S(1)}, s32[512,40]{0,1:T(8,128)}, u32[]{:S(2)}) copy-start(s32[512,40]{0,1:T(8,128)} %param.11) | copy-start | bytes 245764
  2.7 60.0 %copy-start.5 = (bf16[8,1024]{1,0:T(8,128)(2,1)S(1)}, bf16[8,1024]{1,0:T(8,128)(2,1)}, u32[]{:S(2)}) copy-start(bf16[8,1024]{1,0:T(8,128)(2,1)} %expr_ref.1) | copy-start | bytes 49156
  2.7 60.0 %copy-start.6 = (s32[512,8]{0,1:T(8,128)S(1)}, s32[512,8]{0,1:T(8,128)}, u32[]{:S(2)}) copy-start(s32[512,8]{0,1:T(8,128)} %param.10) | copy-start | bytes 49156
  2.7 73.0 %copy-start.3 = (s32[8]{0:T(128)S(1)}, s32[8]{0:T(128)}, u32[]{:S(2)}) copy-start(s32[8]{0:T(128)} %start_ref.3) | copy-start | bytes 100
  63.8 12.0 %collective-permute-start = (bf16[168,1024]{1,0:T(8,128)(2,1)S(1)}, bf16[168,1024]{1,0:T(8,128)(2,1)S(1)}, u32[]{:S(2)}, u32[]{:S(2)}) collective-permute-start(bf16[168,1024]{1,0:T(8,128)(2,1)S(1)} %get-tuple-element.12), channel_id=1, source_target_pairs={{0,1},{1,0},{2,3},{3,2},{4,5},{5,4},{6,7},{7,6},{8,9},{9,8},{10,11... | collective-permute-start | bytes 1032200 | tf_op jit(solution)/shard_map/ppermute | solution.py:366
  66.7 6.6 %collective-permute-start.3 = (bf16[8,1024]{1,0:T(8,128)(2,1)S(1)}, bf16[8,1024]{1,0:T(8,128)(2,1)S(1)}, u32[]{:S(2)}, u32[]{:S(2)}) collective-permute-start(bf16[8,1024]{1,0:T(8,128)(2,1)S(1)} %copy-done.5), channel_id=1, source_target_pairs={{0,2},{2,4},{4,6},{6,8},{8,10},{10,12},{12,14},{14,16},{16,18},{18... | collective-permute-start | bytes 49160 | tf_op jit(solution)/shard_map/ppermute | solution.py:370
  74.4 9.7 %collective-permute-start.4 = (bf16[168,1024]{1,0:T(8,128)(2,1)S(1)}, bf16[168,1024]{1,0:T(8,128)(2,1)S(1)}, u32[]{:S(2)}, u32[]{:S(2)}) collective-permute-start(bf16[168,1024]{1,0:T(8,128)(2,1)S(1)} %get-tuple-element.16), channel_id=1, source_target_pairs={{0,1},{1,0},{2,3},{3,2},{4,5},{5,4},{6,7},{7,6},{8,9},{9,8},{10,11... | collective-permute-start | bytes 1032200 | tf_op jit(solution)/shard_map/ppermute | solution.py:366
  83.8 7.4 %collective-permute-start.2 = (bf16[168,1024]{1,0:T(8,128)(2,1)S(1)}, bf16[168,1024]{1,0:T(8,128)(2,1)S(1)}, u32[]{:S(2)}, u32[]{:S(2)}) collective-permute-start(bf16[168,1024]{1,0:T(8,128)(2,1)S(1)} %get-tuple-element.14), channel_id=1, source_target_pairs={{0,1},{1,0},{2,3},{3,2},{4,5},{5,4},{6,7},{7,6},{8,9},{9,8},{10,11... | collective-permute-start | bytes 1032200 | tf_op jit(solution)/shard_map/ppermute | solution.py:366
  87.9 9.2 %collective-permute-start.6 = (bf16[168,1024]{1,0:T(8,128)(2,1)S(1)}, bf16[168,1024]{1,0:T(8,128)(2,1)S(1)}, u32[]{:S(2)}, u32[]{:S(2)}) collective-permute-start(bf16[168,1024]{1,0:T(8,128)(2,1)S(1)} %spill_product.1), channel_id=1, source_target_pairs={{3,1},{5,3},{7,5},{9,7},{11,9},{13,11},{15,13},{17,15},{19,17},{21... | collective-permute-start | bytes 1032200 | tf_op jit(solution)/shard_map/ppermute | solution.py:378
  89.9 9.8 %collective-permute-start.5 = (bf16[168,1024]{1,0:T(8,128)(2,1)S(1)}, bf16[168,1024]{1,0:T(8,128)(2,1)S(1)}, u32[]{:S(2)}, u32[]{:S(2)}) collective-permute-start(bf16[168,1024]{1,0:T(8,128)(2,1)S(1)} %spill_product.1), channel_id=1, source_target_pairs={{2,1},{4,3},{6,5},{8,7},{10,9},{12,11},{14,13},{16,15},{18,17},{20... | collective-permute-start | bytes 1032200 | tf_op jit(solution)/shard_map/ppermute | solution.py:378

commit v2 on v1

--- a/solution.py
+++ b/solution.py
@@ -19,7 +19,7 @@
 WIDE = 384
 RATIOS = SLOTS * GROUP
 ROWS = RATIOS + 8
-ONES = RATIOS + GROUP
+ALL_VMEM = 67_043_328
 F32 = jnp.float32
 BF16 = jnp.bfloat16
 
@@ -38,31 +38,26 @@
 
 def gather_kernel(block_hbm, counts_hbm, out_ref, block_ref, counts_ref, sems):
     blocks_in = pltpu.make_async_copy(block_hbm, block_ref, sems.at[0])
-    counts_in = pltpu.make_async_copy(counts_hbm, counts_ref, sems.at[1])
+    width = counts_hbm.shape[1]
+    counts_in = pltpu.make_async_copy(counts_hbm, counts_ref.at[:, pl.ds(0, width)], sems.at[1])
     blocks_in.start()
     counts_in.start()
     samples = counts_ref.shape[0]
     owners = out_ref.shape[0]
-    last = counts_ref.shape[1] // LANES - 1
     lane = lax.broadcasted_iota(jnp.int32, (samples, LANES), 1)
     low = lax.broadcasted_iota(jnp.int32, (samples // 2, LANES), 1) < 64
     out_ref[0, 0:40, :] = jnp.zeros((40, LANES), BF16)
     blocks_in.wait()
     counts_in.wait()
 
-    def column(index):
-        start = pl.multiple_of(index * LANES, LANES)
-        return counts_ref[:, pl.ds(start, LANES)].astype(F32)
-
     def owner(o, carry):
         g = []
         for i in range(GENE_DEV):
-            first = block_ref[o * GENE_DEV + i] * SLOTS
-            tile = lax.shift_right_logical(first, 7)
-            inside = first & (LANES - 1)
-            both = jnp.where(
-                lane >= inside, column(tile), column(jnp.minimum(tile + 1, last))
-            )
+            eighths = block_ref[o * GENE_DEV + i] * (SLOTS // 8)
+            inside = (eighths & 15) * 8
+            start = lax.shift_right_logical(eighths, 4) * LANES
+            pair = counts_ref[:, pl.ds(pl.multiple_of(start, LANES), 2 * LANES)].astype(F32)
+            both = jnp.where(lane >= inside, pair[:, :LANES], pair[:, LANES:])
             g.append(pltpu.roll(both, (SLOTS * i - inside) & (LANES - 1), 1))
         a = jnp.where(lane < 40, g[0], jnp.where(lane < 80, g[1], jnp.where(lane < 120, g[2], g[3])))
         b = jnp.where(lane < 32, g[3], jnp.where(lane < 72, g[4], jnp.where(lane < 112, g[5], g[6])))
@@ -87,16 +82,24 @@
         out_specs=VMEM,
         scratch_shapes=[
             pltpu.SMEM(gene_block.shape, jnp.int32),
-            pltpu.VMEM(counts.shape, BF16),
+            pltpu.VMEM((counts.shape[0], counts.shape[1] + LANES), BF16),
             pltpu.SemaphoreType.DMA((2,)),
         ],
-        compiler_params=params(8),
+        compiler_params=pltpu.CompilerParams(vmem_limit_bytes=ALL_VMEM),
         cost_estimate=cost(10_000_000, 1),
         name="gather_blocks",
     )(gene_block, counts)
 
 
-def panel_kernel(behind, recv_ref, expr_ref, sizes_ref, valid_ref, keep_ref, give_ref):
+def panel_kernel(behind, recv_ref, expr_ref, sizes_ref, valid_ref, *refs):
+    hbm, (keep_ref, give_ref), kept, sems = refs[:2], refs[2:4], refs[4:6], refs[6]
+    rows = pl.ds((1 - behind) * SPILL, SPILL)
+    copies = [
+        pltpu.make_async_copy(source.at[rows], to, sems.at[side])
+        for side, (source, to) in enumerate(zip(hbm, kept))
+    ]
+    for copy in copies:
+        copy.start()
     me = jnp.maximum(lax.axis_index("genes") - behind, 0)
     first_core = lax.axis_index("samples") == 0
     first = me * GENE_DEV
@@ -160,19 +163,24 @@
     high_half = jnp.where(row < GROUP, pltpu.roll(expr, GROUP, 0), 1.0)
     keep_ref[RATIOS:ROWS, :] = jnp.where(first_core, low_half, high_half).astype(BF16)
     give_ref[RATIOS:ROWS, :] = jnp.where(first_core, high_half, low_half).astype(BF16)
-
-
-def make_panel(recv, expression, sizes, valid, behind):
-    half = jax.ShapeDtypeStruct((ROWS, expression.shape[1]), BF16)
+    for copy in copies:
+        copy.wait()
+
+
+def make_panel(recv, expression, sizes, valid, doses, behind, limit):
+    samples = expression.shape[1]
+    half = jax.ShapeDtypeStruct((ROWS, samples), BF16)
+    rows = jax.ShapeDtypeStruct((SPILL, samples), BF16)
     return pl.pallas_call(
         functools.partial(panel_kernel, behind),
-        out_shape=(half, half),
-        in_specs=[VMEM] * 4,
-        out_specs=(VMEM, VMEM),
-        compiler_params=params(16),
-        cost_estimate=cost(400_000_000, 1_400_000),
+        out_shape=(half, half, rows, rows),
+        in_specs=[VMEM] * 4 + [HBM, HBM],
+        out_specs=(VMEM,) * 4,
+        scratch_shapes=[pltpu.SemaphoreType.DMA((2,))],
+        compiler_params=params(limit),
+        cost_estimate=cost(400_000_000, 6_000_000),
         name="make_panel",
-    )(recv, expression, sizes, valid)
+    )(recv, expression, sizes, valid, *doses)
 
 
 NT = (((1,), (1,)), ((), ()))
@@ -188,72 +196,66 @@
     return jnp.sum(one, axis=1, keepdims=True), jnp.sum(two, axis=1, keepdims=True)
 
 
-def square_sums(doses):
-    block = doses[0].shape[0]
-    folded = jnp.zeros((block, LANES), F32)
-    for dose in doses:
-        for t in range(dose.shape[1] // LANES):
-            d = dose[:, t * LANES : (t + 1) * LANES].astype(F32)
-            folded = folded + d * d
-    return jnp.sum(jnp.transpose(folded), axis=0, keepdims=True)
+def dose_kernel(count, dose_ref, other_ref, stats_ref):
+    block = dose_ref.shape[0]
+    one, two = jnp.zeros((block, LANES), F32), jnp.zeros((block, LANES), F32)
+    for ref in (dose_ref, other_ref):
+        for t in range(ref.shape[1] // LANES):
+            d = ref[:, t * LANES : (t + 1) * LANES].astype(F32)
+            one, two = one + d, two + d * d
+    sx = jnp.sum(jnp.transpose(one), axis=0, keepdims=True)
+    sxx = jnp.sum(jnp.transpose(two), axis=0, keepdims=True)
+    scale = lax.rsqrt(jnp.maximum(sxx - sx * sx / count, 1.0))
+    row = lax.broadcasted_iota(jnp.int32, (8, block), 0)
+    stats_ref[...] = jnp.where(row == 0, sx, scale)
+
+
+def dose_stats(dosage, other, count):
+    rows, samples = dosage.shape
+    block = 256
+    spec = pl.BlockSpec((block, samples), lambda i: (i, 0))
+    return pl.pallas_call(
+        functools.partial(dose_kernel, count),
+        grid=(rows // block,),
+        out_shape=jax.ShapeDtypeStruct((8, rows), F32),
+        in_specs=[spec, spec],
+        out_specs=pl.BlockSpec((8, block), lambda i: (0, i)),
+        compiler_params=params(8),
+        cost_estimate=cost(20_000_000, 16_000_000),
+        name="dose_stats",
+    )(dosage, other)
 
 
 BLOCK = 256
 
 
-def panel_stats(count, keep_ref, got_ref):
+def correlations(count, keep_ref, got_ref, stats_ref, doses, put):
     sy, syy = row_sums((keep_ref, got_ref))
-    return sy / count, lax.rsqrt(jnp.maximum(syy - sy * sy / count, 1.0))
-
-
-def correlations(count, keep_ref, got_ref, dose, other, stats):
-    cross = lax.dot_general(keep_ref[...], dose[...], NT, preferred_element_type=F32)
-    cross = cross + lax.dot_general(got_ref[...], other[...], NT, preferred_element_type=F32)
-    sx = cross[ONES : ONES + 1]
-    sxx = square_sums((dose, other))
-    dose_scale = lax.rsqrt(jnp.maximum(sxx - sx * sx / count, 1.0))
-    mean, scale = stats
-    return (cross - sx * mean) * dose_scale * scale
-
-
-def streamed(blocks, dose_hbm, other_hbm, doses, sems, body):
-    copies = []
-    for i in range(blocks):
-        rows = pl.ds(i * BLOCK, BLOCK)
-        for side, source in enumerate((dose_hbm, other_hbm)):
-            copy = pltpu.make_async_copy(source.at[rows], doses.at[side, i], sems.at[side, i])
-            copy.start()
-            copies.append(copy)
-    for i in range(blocks):
-        copies[2 * i].wait()
-        copies[2 * i + 1].wait()
-        body(i, doses.at[0, i], doses.at[1, i])
-
-
-def dose_scratch(blocks, samples):
-    return [
-        pltpu.VMEM((2, blocks, BLOCK, samples), BF16),
-        pltpu.SemaphoreType.DMA((2, blocks)),
-    ]
-
-
-def own_product(window_start, keep, got, dosage, other, count):
-    blocks = dosage.shape[0] // BLOCK
+    mean = sy / count
+    scale = lax.rsqrt(jnp.maximum(syy - sy * mean, 1.0))
+    per = SPILL // BLOCK
+    for i in range(per * len(doses)):
+        dose_ref, other_ref = doses[i // per]
+        rows = slice(i % per * BLOCK, (i % per + 1) * BLOCK)
+        lanes = slice(i * BLOCK, (i + 1) * BLOCK)
+        cross = lax.dot_general(keep_ref[...], dose_ref[rows], NT, preferred_element_type=F32)
+        cross = cross + lax.dot_general(
+            got_ref[...], other_ref[rows], NT, preferred_element_type=F32
+        )
+        put(lanes, (cross - stats_ref[0:1, lanes] * mean) * stats_ref[1:2, lanes] * scale)
+
+
+def own_product(window_start, keep, got, stats, near, far, count):
     side = jax.ShapeDtypeStruct((ROWS, HALF), BF16)
 
-    def kernel(
-        start_ref, keep_ref, got_ref, dose_hbm, other_hbm, mine_ref, theirs_ref, doses, sems, wide
-    ):
+    def kernel(start_ref, keep_ref, got_ref, stats_ref, *refs):
+        doses, (mine_ref, theirs_ref, wide) = (refs[0:2], refs[2:4]), refs[4:]
         core = lax.axis_index("samples")
-        stats = []
-
-        def body(i, dose, other):
-            if i == 0:
-                stats.append(panel_stats(count, keep_ref, got_ref))
-            lanes = slice(i * BLOCK, (i + 1) * BLOCK)
-            wide[:, lanes] = correlations(count, keep_ref, got_ref, dose, other, stats[0])
-
-        streamed(blocks, dose_hbm, other_hbm, doses, sems, body)
+
+        def put(lanes, values):
+            wide[:, lanes] = values
+
+        correlations(count, keep_ref, got_ref, stats_ref, doses, put)
         wide[:, W : W + SPILL] = jnp.zeros((ROWS, SPILL), F32)
         for ref, side in ((theirs_ref, 1 - core), (mine_ref, core)):
             last = []
@@ -269,41 +271,31 @@
     return pl.pallas_call(
         kernel,
         out_shape=(side, side),
-        in_specs=[SMEM, VMEM, VMEM, HBM, HBM],
+        in_specs=[SMEM] + [VMEM] * 7,
         out_specs=(VMEM, VMEM),
-        scratch_shapes=dose_scratch(blocks, dosage.shape[1])
-        + [pltpu.VMEM((ROWS, W + SPILL), F32)],
-        compiler_params=params(24),
-        cost_estimate=cost(1_500_000_000, 1),
+        scratch_shapes=[pltpu.VMEM((ROWS, W + SPILL), F32)],
+        compiler_params=params(16),
+        cost_estimate=cost(1_500_000_000, 12_000_000),
         name="own_product",
-    )(window_start, keep, got, dosage, other)
-
-
-def spill_product(keep, got, dosage, other, count):
-    blocks = SPILL // BLOCK
-
-    def kernel(keep_ref, got_ref, dose_hbm, other_hbm, out_ref, doses, sems):
-        stats = []
-
-        def body(i, dose, other):
-            if i == 0:
-                stats.append(panel_stats(count, keep_ref, got_ref))
-            lanes = slice(i * BLOCK, (i + 1) * BLOCK)
-            value = correlations(count, keep_ref, got_ref, dose, other, stats[0])
-            out_ref[:, lanes] = value.astype(BF16)
-
-        streamed(blocks, dose_hbm, other_hbm, doses, sems, body)
+    )(window_start, keep, got, stats, *near, *far)
+
+
+def spill_product(keep, got, stats, near, count):
+    def kernel(keep_ref, got_ref, stats_ref, dose_ref, other_ref, out_ref):
+        def put(lanes, values):
+            out_ref[:, lanes] = values.astype(BF16)
+
+        correlations(count, keep_ref, got_ref, stats_ref, ((dose_ref, other_ref),), put)
 
     return pl.pallas_call(
         kernel,
         out_shape=jax.ShapeDtypeStruct((ROWS, SPILL), BF16),
-        in_specs=[VMEM, VMEM, HBM, HBM],
+        in_specs=[VMEM] * 5,
         out_specs=VMEM,
-        scratch_shapes=dose_scratch(blocks, dosage.shape[1]),
         compiler_params=params(16),
-        cost_estimate=cost(700_000_000, 1),
+        cost_estimate=cost(700_000_000, 6_000_000),
         name="spill_product",
-    )(keep, got, dosage, other)
+    )(keep, got, stats, *near)
 
 
 def merge_kernel(start_ref, mine_ref, other_ref, back0, back1, out_ref, wide, rows48):
@@ -370,16 +362,19 @@
     prev_expression = lax.ppermute(expression, "genes", onward)
     recv = lax.all_to_all(blocks, "genes", 0, 0, tiled=True)
 
-    keep, give = make_panel(recv, prev_expression, sizes, valid, 1)
+    stats = dose_stats(dosage, other_dose, count)
+    doses = (dosage, other_dose)
+
+    keep, give, *near = make_panel(recv, prev_expression, sizes, valid, doses, 1, 44)
     got = exchanged(give)
-    piece = spill_product(keep, got, dosage, other_dose, count)
+    piece = spill_product(keep, got, stats, near, count)
     back = []
     for c in range(cores):
         back.append(lax.ppermute(piece, ("genes", "samples"), home[c]))
 
-    keep, give = make_panel(recv, expression, sizes, valid, 0)
+    keep, give, *far = make_panel(recv, expression, sizes, valid, doses, 0, 40)
     got = exchanged(give)
-    mine, theirs = own_product(window_start, keep, got, dosage, other_dose, count)
+    mine, theirs = own_product(window_start, keep, got, stats, near, far, count)
     other = exchanged(theirs)
     out = merge(window_start, mine, other, back)
     return jnp.transpose(out, (1, 0, 2))

time: 103 us -> 109 us (1.058)
  Pallas kernels: 19.8 us -> 22.9 us
  blocking collectives: 56.2 us -> 58.2 us
    pallas_call x2, Pallas kernels: 2.13 us -> 4.97 us  [make_panel(): pl.pallas_call(functools.partial(panel_kernel, behind), out_shape=(half,...]
    pallas_call x1, Pallas kernels: 3.75 us -> 1.58 us  [spill_product(): pl.pallas_call(kernel, out_shape=jax.ShapeDtypeStruct((ROWS, SPILL), BF16...]
    all_to_all x1, blocking collectives: 56.2 us -> 58.2 us  [shards(): recv = lax.all_to_all(blocks, 'genes', 0, 0, tiled=True)]
    pallas_call x1 -> x2, Pallas kernels: 8.04 us -> 9.78 us  [the longest x1 6.14 us: dose_stats(): pl.pallas_call(functools.partial(dose_kernel, count), grid=(rows // block...]
    unnamed x14 -> x12, local copies, waits for them, and re-layouts: 2.09 us -> 2.21 us
where the time goes in v2:
time: 109 us; the launch traced here: 108 us
  blocking collectives  58.2 us (53%)
  Pallas kernels  22.9 us (21%)
  waiting for transfers between devices  12.5 us (11%)
  starting transfers between devices  11.6 us (11%)
  local copies, waits for them, and re-layouts  2.21 us (2%)
    all_to_all x1, blocking collectives, shards(): recv = lax.all_to_all(blocks, 'genes', 0, 0, tiled=True)  58.2 us
    ppermute x2, waiting for transfers between devices, shards(): back.append(lax.ppermute(piece, ('genes', 'samples'), home[c]))  9 us
    pallas_call x1, Pallas kernels, dose_stats(): pl.pallas_call(functools.partial(dose_kernel, count), grid=(rows // block...  6.14 us
    ppermute x4, starting transfers between devices, exchanged(): return lax.ppermute(x, 'samples', swap)  5.2 us
    pallas_call x2, Pallas kernels, make_panel(): pl.pallas_call(functools.partial(panel_kernel, behind), out_shape=(half,...  4.97 us
    pallas_call x1, Pallas kernels, gather_blocks(): pl.pallas_call(gather_kernel, out_shape=jax.ShapeDtypeStruct((owners, 80,...  4.46 us
    pallas_call x1, Pallas kernels, own_product(): pl.pallas_call(kernel, out_shape=(side, side), in_specs=[SMEM] + [VMEM] *...  3.64 us
    ppermute x1, waiting for transfers between devices, shards(): prev_expression = lax.ppermute(expression, 'genes', onward)  3.44 us
  transfers between devices with their start and end apart: 7, of which 3 were waited for; matrix products, arithmetic and copies ran while one was open for 0% of the time, Pallas kernels for 17%

profile of v2, /device:TPU:515, one launch (start us, length us, event | category | flops | bytes accessed | tf_op | source)
XLA Modules:
  0.0 107.6 jit_solution(15849688599300658600)
XLA Ops:
  0.0 0.6 collective-permute-start
  0.6 4.5 %gather_blocks.1 = bf16[64,80,128]{2,1,0:T(8,128)(2,1)} custom-call(s32[512]{0:T(512)} %block_hbm.1, bf16[16,20480]{1,0:T(8,128)(2,1)} %counts_hbm.1), custom_call_target="tpu_custom_call" | custom-call | flops 10000000 | bytes 1 | tf_op jit(solution)/shard_map/gather_blocks/pallas_call | solution.py:78
  5.1 0.0 copy-start.2
  5.1 0.0 copy-start.3
  5.1 0.0 copy-start.4
  5.1 58.2 %all_to_all.5.recv_ref = bf16[64,80,128]{2,1,0:T(8,128)(2,1)S(1)} all-to-all(bf16[64,80,128]{2,1,0:T(8,128)(2,1)} %gather_blocks.1), channel_id=1, replica_groups=mesh['parts'=2,'genes'=64,'samples'=2] {'genes'}, dimensions={0} | all-to-all | bytes 2621440 | tf_op jit(solution)/shard_map/all_to_all | solution.py:363
  63.4 0.0 collective-permute-done.refs_1_.other_ref
  63.4 0.0 copy-done.2
  63.4 0.0 copy-done.3
  63.4 0.0 copy-done.4
  63.4 0.0 copy-start
  63.4 2.2 %copy-done = bf16[2048,1024]{1,0:T(8,128)(2,1)S(1)} copy-done((bf16[2048,1024]{1,0:T(8,128)(2,1)S(1)}, bf16[2048,1024]{1,0:T(8,128)(2,1)}, u32[]{:S(2)}) %copy-start) | copy-done | bytes 4194328
  65.6 2.6 %make_panel.2 = (bf16[168,1024]{1,0:T(8,128)(2,1)S(1)}, bf16[168,1024]{1,0:T(8,128)(2,1)S(1)}, bf16[1024,1024]{1,0:T(8,128)(2,1)S(1)}, bf16[1024,1024]{1,0:T(8,128)(2,1)S(1)}) custom-call(bf16[64,80,128]{2,1,0:T(8,128)(2,1)S(1)} %all_to_all.5.recv_ref, bf16[8,1024]{1,0:T(8,128)(2,1)S(1)} %copy-done.4, s32[8,512]{1,0:T(8,128)S(1)} %bitcast.5, ...), custom_call_target="tpu_custom_call" | custom-call | flops 400000000 | bytes 6000000 | tf_op jit(solution)/shard_map/make_panel/pallas_call | solution.py:174
  68.1 2.3 %collective-permute-start.1 = (bf16[168,1024]{1,0:T(8,128)(2,1)S(1)}, bf16[168,1024]{1,0:T(8,128)(2,1)S(1)}, u32[]{:S(2)}, u32[]{:S(2)}) collective-permute-start(bf16[168,1024]{1,0:T(8,128)(2,1)S(1)} %get-tuple-element.16), channel_id=1, source_target_pairs={{0,1},{1,0},{2,3},{3,2},{4,5},{5,4},{6,7},{7,6},{8,9},{9,8},{10,11... | collective-permute-start | bytes 1032200 | tf_op jit(solution)/shard_map/ppermute | solution.py:358
  70.4 3.2 %collective-permute-start.2 = (bf16[8,1024]{1,0:T(8,128)(2,1)S(1)}, bf16[8,1024]{1,0:T(8,128)(2,1)S(1)}, u32[]{:S(2)}, u32[]{:S(2)}) collective-permute-start(bf16[8,1024]{1,0:T(8,128)(2,1)S(1)} %copy-done.4), channel_id=1, source_target_pairs={{0,2},{2,4},{4,6},{6,8},{8,10},{10,12},{12,14},{14,16},{16,18},{18... | collective-permute-start | bytes 49160 | tf_op jit(solution)/shard_map/ppermute | solution.py:362
  73.6 3.4 %collective-permute-done.2.expr_ref = bf16[8,1024]{1,0:T(8,128)(2,1)S(1)} collective-permute-done((bf16[8,1024]{1,0:T(8,128)(2,1)S(1)}, bf16[8,1024]{1,0:T(8,128)(2,1)S(1)}, u32[]{:S(2)}, u32[]{:S(2)}) %collective-permute-start.2) | collective-permute-done | bytes 16416 | tf_op jit(solution)/shard_map/ppermute | solution.py:362
  77.0 0.0 copy-start.1
  77.0 2.4 %make_panel.3 = (bf16[168,1024]{1,0:T(8,128)(2,1)S(1)}, bf16[168,1024]{1,0:T(8,128)(2,1)S(1)}, bf16[1024,1024]{1,0:T(8,128)(2,1)S(1)}, bf16[1024,1024]{1,0:T(8,128)(2,1)S(1)}) custom-call(bf16[64,80,128]{2,1,0:T(8,128)(2,1)S(1)} %all_to_all.5.recv_ref, bf16[8,1024]{1,0:T(8,128)(2,1)S(1)} %collective-permute-done.2.expr_ref, s32[8,512]{1,0:T(8,128)S(1)} %bitcast.6, ...), custom_call_target="tpu_custom_call" | custom-call | flops 400000000 | bytes 6000000 | tf_op jit(solution)/shard_map/make_panel/pallas_call | solution.py:174
  79.4 0.0 copy-start.5
  79.4 1.3 %collective-permute-start.4 = (bf16[168,1024]{1,0:T(8,128)(2,1)S(1)}, bf16[168,1024]{1,0:T(8,128)(2,1)S(1)}, u32[]{:S(2)}, u32[]{:S(2)}) collective-permute-start(bf16[168,1024]{1,0:T(8,128)(2,1)S(1)} %get-tuple-element.24), channel_id=1, source_target_pairs={{0,1},{1,0},{2,3},{3,2},{4,5},{5,4},{6,7},{7,6},{8,9},{9,8},{10,11... | collective-permute-start | bytes 1032200 | tf_op jit(solution)/shard_map/ppermute | solution.py:358
  80.8 0.0 copy-done.1
  80.8 6.1 %dose_stats.1.stats_ref = f32[8,2048]{1,0:T(8,128)S(1)} custom-call(bf16[2048,1024]{1,0:T(8,128)(2,1)S(1)} %copy-done.1, bf16[2048,1024]{1,0:T(8,128)(2,1)} %collective-permute-done.refs_1_.other_ref), custom_call_target="tpu_custom_call" | custom-call | flops 20000000 | bytes 16000000 | tf_op jit(solution)/shard_map/dose_stats/pallas_call | solution.py:217
  86.9 0.0 collective-permute-done.1.got_ref
  86.9 0.0 copy-done.5
  86.9 3.6 %own_product.1 = (bf16[168,1024]{1,0:T(8,128)(2,1)S(1)}, bf16[168,1024]{1,0:T(8,128)(2,1)S(1)}) custom-call(s32[8]{0:T(128)S(1)} %copy-done.5, bf16[168,1024]{1,0:T(8,128)(2,1)S(1)} %get-tuple-element.15.keep_ref, bf16[168,1024]{1,0:T(8,128)(2,1)S(1)} %collective-permute-done.1.got_ref, f32[8,2048]{1,0:T(8,128)S(1)} %dose_stats.1.stats_ref, ...), custom_call_target="tpu_custom_call" | custom-call | flops 1500000000 | bytes 12000000 | tf_op jit(solution)/shard_map/own_product/pallas_call | solution.py:271
  90.6 1.0 collective-permute-start.3
  91.6 0.0 collective-permute-done.4.got_ref
  91.6 1.6 %spill_product.1 = bf16[168,1024]{1,0:T(8,128)(2,1)S(1)} custom-call(bf16[168,1024]{1,0:T(8,128)(2,1)S(1)} %get-tuple-element.23.keep_ref, bf16[168,1024]{1,0:T(8,128)(2,1)S(1)} %collective-permute-done.4.got_ref, f32[8,2048]{1,0:T(8,128)S(1)} %dose_stats.1.stats_ref, bf16[1024,1024]{1,0:T(8,128)(2,1)S(1)} %get-tuple-element.17.refs_0_.dose_ref, ...), custom_call_target="tpu_custom_call" | custom-call | flops 700000000 | bytes 6000000 | tf_op jit(solution)/shard_map/spill_product/pallas_call | solution.py:290
  93.2 1.3 %collective-permute-start.5 = (bf16[168,1024]{1,0:T(8,128)(2,1)S(1)}, bf16[168,1024]{1,0:T(8,128)(2,1)S(1)}, u32[]{:S(2)}, u32[]{:S(2)}) collective-permute-start(bf16[168,1024]{1,0:T(8,128)(2,1)S(1)} %spill_product.1), channel_id=1, source_target_pairs={{2,1},{4,3},{6,5},{8,7},{10,9},{12,11},{14,13},{16,15},{18,17},{20... | collective-permute-start | bytes 1032200 | tf_op jit(solution)/shard_map/ppermute | solution.py:373
  94.5 2.0 %collective-permute-start.6 = (bf16[168,1024]{1,0:T(8,128)(2,1)S(1)}, bf16[168,1024]{1,0:T(8,128)(2,1)S(1)}, u32[]{:S(2)}, u32[]{:S(2)}) collective-permute-start(bf16[168,1024]{1,0:T(8,128)(2,1)S(1)} %spill_product.1), channel_id=1, source_target_pairs={{3,1},{5,3},{7,5},{9,7},{11,9},{13,11},{15,13},{17,15},{19,17},{21... | collective-permute-start | bytes 1032200 | tf_op jit(solution)/shard_map/ppermute | solution.py:373
  96.5 0.0 collective-permute-done.3.other_ref
  96.5 8.3 %collective-permute-done.5.back0 = bf16[168,1024]{1,0:T(8,128)(2,1)S(1)} collective-permute-done((bf16[168,1024]{1,0:T(8,128)(2,1)S(1)}, bf16[168,1024]{1,0:T(8,128)(2,1)S(1)}, u32[]{:S(2)}, u32[]{:S(2)}) %collective-permute-start.5) | collective-permute-done | bytes 344096 | tf_op jit(solution)/shard_map/ppermute | solution.py:373
  104.7 0.7 collective-permute-done.6.back1
  105.5 2.1 %merge_windows.1 = bf16[41,8,1024]{2,1,0:T(8,128)(2,1)} custom-call(s32[8]{0:T(128)S(1)} %copy-done.5, bf16[168,1024]{1,0:T(8,128)(2,1)S(1)} %get-tuple-element.21.mine_ref, bf16[168,1024]{1,0:T(8,128)(2,1)S(1)} %collective-permute-done.3.other_ref, bf16[168,1024]{1,0:T(8,128)(2,1)S(1)} %collective-permute-done.5.back0, ...), custom_call_target="tpu_custom_call" | custom-call | flops 2000000 | bytes 3500000 | tf_op jit(solution)/shard_map/merge_windows/pallas_call | solution.py:330
Async XLA Ops:
  0.0 63.4 %collective-permute-start = (bf16[2048,1024]{1,0:T(8,128)(2,1)}, bf16[2048,1024]{1,0:T(8,128)(2,1)}, u32[]{:S(2)}, u32[]{:S(2)}) collective-permute-start(bf16[2048,1024]{1,0:T(8,128)(2,1)} %refs_0_.3), channel_id=1, source_target_pairs={{0,1},{1,0},{2,3},{3,2},{4,5},{5,4},{6,7},{7,6},{8,9},{9,8},{10,11... | collective-permute-start | bytes 12582920 | tf_op jit(solution)/shard_map/ppermute | solution.py:358
  5.1 58.3 %copy-start.2 = (s32[512,40]{0,1:T(8,128)S(1)}, s32[512,40]{0,1:T(8,128)}, u32[]{:S(2)}) copy-start(s32[512,40]{0,1:T(8,128)} %param.11) | copy-start | bytes 245764
  5.1 58.3 %copy-start.3 = (s32[512,8]{0,1:T(8,128)S(1)}, s32[512,8]{0,1:T(8,128)}, u32[]{:S(2)}) copy-start(s32[512,8]{0,1:T(8,128)} %param.10) | copy-start | bytes 49156
  5.1 58.3 %copy-start.4 = (bf16[8,1024]{1,0:T(8,128)(2,1)S(1)}, bf16[8,1024]{1,0:T(8,128)(2,1)}, u32[]{:S(2)}) copy-start(bf16[8,1024]{1,0:T(8,128)(2,1)} %expr_ref.1) | copy-start | bytes 49156
  63.4 2.2 %copy-start = (bf16[2048,1024]{1,0:T(8,128)(2,1)S(1)}, bf16[2048,1024]{1,0:T(8,128)(2,1)}, u32[]{:S(2)}) copy-start(bf16[2048,1024]{1,0:T(8,128)(2,1)} %refs_0_.3) | copy-start | bytes 12582916
  68.1 18.8 %collective-permute-start.1 = (bf16[168,1024]{1,0:T(8,128)(2,1)S(1)}, bf16[168,1024]{1,0:T(8,128)(2,1)S(1)}, u32[]{:S(2)}, u32[]{:S(2)}) collective-permute-start(bf16[168,1024]{1,0:T(8,128)(2,1)S(1)} %get-tuple-element.16), channel_id=1, source_target_pairs={{0,1},{1,0},{2,3},{3,2},{4,5},{5,4},{6,7},{7,6},{8,9},{9,8},{10,11... | collective-permute-start | bytes 1032200 | tf_op jit(solution)/shard_map/ppermute | solution.py:358
  70.4 6.6 %collective-permute-start.2 = (bf16[8,1024]{1,0:T(8,128)(2,1)S(1)}, bf16[8,1024]{1,0:T(8,128)(2,1)S(1)}, u32[]{:S(2)}, u32[]{:S(2)}) collective-permute-start(bf16[8,1024]{1,0:T(8,128)(2,1)S(1)} %copy-done.4), channel_id=1, source_target_pairs={{0,2},{2,4},{4,6},{6,8},{8,10},{10,12},{12,14},{14,16},{16,18},{18... | collective-permute-start | bytes 49160 | tf_op jit(solution)/shard_map/ppermute | solution.py:362
  77.0 3.7 %copy-start.1 = (bf16[2048,1024]{1,0:T(8,128)(2,1)S(1)}, bf16[2048,1024]{1,0:T(8,128)(2,1)}, u32[]{:S(2)}) copy-start(bf16[2048,1024]{1,0:T(8,128)(2,1)} %refs_0_.3) | copy-start | bytes 12582916
  79.4 7.5 %copy-start.5 = (s32[8]{0:T(128)S(1)}, s32[8]{0:T(128)}, u32[]{:S(2)}) copy-start(s32[8]{0:T(128)} %start_ref.3) | copy-start | bytes 100
  79.4 12.2 %collective-permute-start.4 = (bf16[168,1024]{1,0:T(8,128)(2,1)S(1)}, bf16[168,1024]{1,0:T(8,128)(2,1)S(1)}, u32[]{:S(2)}, u32[]{:S(2)}) collective-permute-start(bf16[168,1024]{1,0:T(8,128)(2,1)S(1)} %get-tuple-element.24), channel_id=1, source_target_pairs={{0,1},{1,0},{2,3},{3,2},{4,5},{5,4},{6,7},{7,6},{8,9},{9,8},{10,11... | collective-permute-start | bytes 1032200 | tf_op jit(solution)/shard_map/ppermute | solution.py:358
  90.6 5.9 %collective-permute-start.3 = (bf16[168,1024]{1,0:T(8,128)(2,1)S(1)}, bf16[168,1024]{1,0:T(8,128)(2,1)S(1)}, u32[]{:S(2)}, u32[]{:S(2)}) collective-permute-start(bf16[168,1024]{1,0:T(8,128)(2,1)S(1)} %get-tuple-element.22), channel_id=1, source_target_pairs={{0,1},{1,0},{2,3},{3,2},{4,5},{5,4},{6,7},{7,6},{8,9},{9,8},{10,11... | collective-permute-start | bytes 1032200 | tf_op jit(solution)/shard_map/ppermute | solution.py:358
  93.2 11.5 %collective-permute-start.5 = (bf16[168,1024]{1,0:T(8,128)(2,1)S(1)}, bf16[168,1024]{1,0:T(8,128)(2,1)S(1)}, u32[]{:S(2)}, u32[]{:S(2)}) collective-permute-start(bf16[168,1024]{1,0:T(8,128)(2,1)S(1)} %spill_product.1), channel_id=1, source_target_pairs={{2,1},{4,3},{6,5},{8,7},{10,9},{12,11},{14,13},{16,15},{18,17},{20... | collective-permute-start | bytes 1032200 | tf_op jit(solution)/shard_map/ppermute | solution.py:373
  94.5 11.0 %collective-permute-start.6 = (bf16[168,1024]{1,0:T(8,128)(2,1)S(1)}, bf16[168,1024]{1,0:T(8,128)(2,1)S(1)}, u32[]{:S(2)}, u32[]{:S(2)}) collective-permute-start(bf16[168,1024]{1,0:T(8,128)(2,1)S(1)} %spill_product.1), channel_id=1, source_target_pairs={{3,1},{5,3},{7,5},{9,7},{11,9},{13,11},{15,13},{17,15},{19,17},{21... | collective-permute-start | bytes 1032200 | tf_op jit(solution)/shard_map/ppermute | solution.py:373

commit v3 on v2

--- a/solution.py
+++ b/solution.py
@@ -20,6 +20,7 @@
 RATIOS = SLOTS * GROUP
 ROWS = RATIOS + 8
 ALL_VMEM = 67_043_328
+LIM = 44
 F32 = jnp.float32
 BF16 = jnp.bfloat16
 
@@ -43,10 +44,8 @@
     blocks_in.start()
     counts_in.start()
     samples = counts_ref.shape[0]
-    owners = out_ref.shape[0]
     lane = lax.broadcasted_iota(jnp.int32, (samples, LANES), 1)
     low = lax.broadcasted_iota(jnp.int32, (samples // 2, LANES), 1) < 64
-    out_ref[0, 0:40, :] = jnp.zeros((40, LANES), BF16)
     blocks_in.wait()
     counts_in.wait()
 
@@ -63,21 +62,18 @@
         b = jnp.where(lane < 32, g[3], jnp.where(lane < 72, g[4], jnp.where(lane < 112, g[5], g[6])))
         c = jnp.where(lane < 24, g[6], g[7])
         packed = jnp.where(low, c[: samples // 2], pltpu.roll(c[samples // 2 :], 64, 1))
-        after = jnp.minimum(o + 1, owners - 1)
-        for at, row in ((after, 0), (o, 40)):
-            out_ref[at, row : row + 16, :] = a.astype(BF16)
-            out_ref[at, row + 16 : row + 32, :] = b.astype(BF16)
-            out_ref[at, row + 32 : row + 40, :] = packed.astype(BF16)
+        out_ref[o, 0:16, :] = a.astype(BF16)
+        out_ref[o, 16:32, :] = b.astype(BF16)
+        out_ref[o, 32:40, :] = packed.astype(BF16)
         return carry
 
-    owner(owners - 1, 0)
-    lax.fori_loop(0, owners - 1, owner, 0, unroll=9)
+    lax.fori_loop(0, out_ref.shape[0], owner, 0, unroll=8)
 
 
 def gather_blocks(gene_block, counts, owners):
     return pl.pallas_call(
         gather_kernel,
-        out_shape=jax.ShapeDtypeStruct((owners, 80, LANES), BF16),
+        out_shape=jax.ShapeDtypeStruct((owners, 40, LANES), BF16),
         in_specs=[HBM, HBM],
         out_specs=VMEM,
         scratch_shapes=[
@@ -91,17 +87,9 @@
     )(gene_block, counts)
 
 
-def panel_kernel(behind, recv_ref, expr_ref, sizes_ref, valid_ref, *refs):
-    hbm, (keep_ref, give_ref), kept, sems = refs[:2], refs[2:4], refs[4:6], refs[6]
-    rows = pl.ds((1 - behind) * SPILL, SPILL)
-    copies = [
-        pltpu.make_async_copy(source.at[rows], to, sems.at[side])
-        for side, (source, to) in enumerate(zip(hbm, kept))
-    ]
-    for copy in copies:
-        copy.start()
-    me = jnp.maximum(lax.axis_index("genes") - behind, 0)
-    first_core = lax.axis_index("samples") == 0
+def tables_kernel(expr_ref, sizes_ref, valid_ref, same_ref, live_ref, kept_ref):
+    kept_ref[...] = expr_ref[...]
+    me = lax.axis_index("genes")
     first = me * GENE_DEV
     start = pl.multiple_of(first // LANES * LANES, LANES)
     back = (LANES - first % LANES) & (LANES - 1)
@@ -138,12 +126,33 @@
 
     k = lax.broadcasted_iota(jnp.int32, (WIDE, WIDE), 0).astype(F32)
     inside = (k >= base + low) & (k < base + high)
-    same = jnp.where(inside & (k < float(SLOTS * GENE_DEV)), 1.0, 0.0).astype(BF16)
-
+    same_ref[...] = jnp.where(inside & (k < float(SLOTS * GENE_DEV)), 1.0, 0.0).astype(BF16)
+    live_ref[...] = jnp.broadcast_to(live, (8, WIDE))
+
+
+def make_tables(expression, sizes, valid):
+    return pl.pallas_call(
+        tables_kernel,
+        out_shape=(
+            jax.ShapeDtypeStruct((WIDE, WIDE), BF16),
+            jax.ShapeDtypeStruct((8, WIDE), F32),
+            jax.ShapeDtypeStruct(expression.shape, expression.dtype),
+        ),
+        in_specs=[VMEM] * 3,
+        out_specs=(VMEM,) * 3,
+        compiler_params=params(16),
+        cost_estimate=cost(10_000_000, 1_000_000),
+        name="make_tables",
+    )(expression, sizes, valid)
+
+
+def panel_kernel(recv_ref, same_ref, live_ref, expr_ref, keep_ref, give_ref):
+    first_core = lax.axis_index("samples") == 0
+    live = live_ref[0:1, :]
+    same = same_ref[...]
     per = LANES // 16
     for t in range(recv_ref.shape[0] // per):
-        owned = 40 * (1 - behind)
-        piece = recv_ref[t * per : (t + 1) * per, owned : owned + 40, :].astype(F32)
+        piece = recv_ref[t * per : (t + 1) * per].astype(F32)
         a = piece[:, 0:16, :].reshape(LANES, LANES)
         b = piece[:, 16:32, :].reshape(LANES, LANES)
         c = piece[:, 32:40, :]
@@ -163,24 +172,19 @@
     high_half = jnp.where(row < GROUP, pltpu.roll(expr, GROUP, 0), 1.0)
     keep_ref[RATIOS:ROWS, :] = jnp.where(first_core, low_half, high_half).astype(BF16)
     give_ref[RATIOS:ROWS, :] = jnp.where(first_core, high_half, low_half).astype(BF16)
-    for copy in copies:
-        copy.wait()
-
-
-def make_panel(recv, expression, sizes, valid, doses, behind, limit):
-    samples = expression.shape[1]
-    half = jax.ShapeDtypeStruct((ROWS, samples), BF16)
-    rows = jax.ShapeDtypeStruct((SPILL, samples), BF16)
-    return pl.pallas_call(
-        functools.partial(panel_kernel, behind),
-        out_shape=(half, half, rows, rows),
-        in_specs=[VMEM] * 4 + [HBM, HBM],
-        out_specs=(VMEM,) * 4,
-        scratch_shapes=[pltpu.SemaphoreType.DMA((2,))],
-        compiler_params=params(limit),
-        cost_estimate=cost(400_000_000, 6_000_000),
+
+
+def make_panel(recv, tables):
+    half = jax.ShapeDtypeStruct((ROWS, tables[2].shape[1]), BF16)
+    return pl.pallas_call(
+        panel_kernel,
+        out_shape=(half, half),
+        in_specs=[VMEM] * 4,
+        out_specs=(VMEM, VMEM),
+        compiler_params=params(16),
+        cost_estimate=cost(400_000_000, 2_000_000),
         name="make_panel",
-    )(recv, expression, sizes, valid, *doses)
+    )(recv, *tables)
 
 
 NT = (((1,), (1,)), ((), ()))
@@ -196,66 +200,77 @@
     return jnp.sum(one, axis=1, keepdims=True), jnp.sum(two, axis=1, keepdims=True)
 
 
-def dose_kernel(count, dose_ref, other_ref, stats_ref):
-    block = dose_ref.shape[0]
-    one, two = jnp.zeros((block, LANES), F32), jnp.zeros((block, LANES), F32)
-    for ref in (dose_ref, other_ref):
-        for t in range(ref.shape[1] // LANES):
-            d = ref[:, t * LANES : (t + 1) * LANES].astype(F32)
-            one, two = one + d, two + d * d
-    sx = jnp.sum(jnp.transpose(one), axis=0, keepdims=True)
-    sxx = jnp.sum(jnp.transpose(two), axis=0, keepdims=True)
-    scale = lax.rsqrt(jnp.maximum(sxx - sx * sx / count, 1.0))
-    row = lax.broadcasted_iota(jnp.int32, (8, block), 0)
-    stats_ref[...] = jnp.where(row == 0, sx, scale)
+BLOCK = 256
+
+
+def dose_kernel(count, dose_hbm, other_hbm, dose_ref, other_ref, stats_ref, sems):
+    blocks = dose_ref.shape[0] // BLOCK
+    copies = [
+        [
+            pltpu.make_async_copy(
+                source.at[pl.ds(i * BLOCK, BLOCK)], to.at[pl.ds(i * BLOCK, BLOCK)], sems.at[side, i]
+            )
+            for side, (source, to) in enumerate(((dose_hbm, dose_ref), (other_hbm, other_ref)))
+        ]
+        for i in range(blocks)
+    ]
+    for pair in copies:
+        for copy in pair:
+            copy.start()
+    row = lax.broadcasted_iota(jnp.int32, (8, BLOCK), 0)
+    for i, pair in enumerate(copies):
+        one, two = jnp.zeros((BLOCK, LANES), F32), jnp.zeros((BLOCK, LANES), F32)
+        for copy, ref in zip(pair, (dose_ref, other_ref)):
+            copy.wait()
+            for t in range(ref.shape[1] // LANES):
+                d = ref[i * BLOCK : (i + 1) * BLOCK, t * LANES : (t + 1) * LANES].astype(F32)
+                one, two = one + d, two + d * d
+        sx = jnp.sum(jnp.transpose(one), axis=0, keepdims=True)
+        sxx = jnp.sum(jnp.transpose(two), axis=0, keepdims=True)
+        scale = lax.rsqrt(jnp.maximum(sxx - sx * sx / count, 1.0))
+        stats_ref[:, i * BLOCK : (i + 1) * BLOCK] = jnp.where(row == 0, sx, scale)
 
 
 def dose_stats(dosage, other, count):
-    rows, samples = dosage.shape
-    block = 256
-    spec = pl.BlockSpec((block, samples), lambda i: (i, 0))
+    rows = dosage.shape[0]
+    same = jax.ShapeDtypeStruct(dosage.shape, dosage.dtype)
     return pl.pallas_call(
         functools.partial(dose_kernel, count),
-        grid=(rows // block,),
-        out_shape=jax.ShapeDtypeStruct((8, rows), F32),
-        in_specs=[spec, spec],
-        out_specs=pl.BlockSpec((8, block), lambda i: (0, i)),
-        compiler_params=params(8),
+        out_shape=(same, same, jax.ShapeDtypeStruct((8, rows), F32)),
+        in_specs=[HBM, HBM],
+        out_specs=(VMEM,) * 3,
+        scratch_shapes=[pltpu.SemaphoreType.DMA((2, rows // BLOCK))],
+        compiler_params=params(LIM),
         cost_estimate=cost(20_000_000, 16_000_000),
         name="dose_stats",
     )(dosage, other)
 
 
-BLOCK = 256
-
-
-def correlations(count, keep_ref, got_ref, stats_ref, doses, put):
+def correlations(count, keep_ref, got_ref, stats_ref, doses, variants, put):
     sy, syy = row_sums((keep_ref, got_ref))
     mean = sy / count
     scale = lax.rsqrt(jnp.maximum(syy - sy * mean, 1.0))
-    per = SPILL // BLOCK
-    for i in range(per * len(doses)):
-        dose_ref, other_ref = doses[i // per]
-        rows = slice(i % per * BLOCK, (i % per + 1) * BLOCK)
+    dose_ref, other_ref = doses
+    for i in range(variants // BLOCK):
         lanes = slice(i * BLOCK, (i + 1) * BLOCK)
-        cross = lax.dot_general(keep_ref[...], dose_ref[rows], NT, preferred_element_type=F32)
+        cross = lax.dot_general(keep_ref[...], dose_ref[lanes], NT, preferred_element_type=F32)
         cross = cross + lax.dot_general(
-            got_ref[...], other_ref[rows], NT, preferred_element_type=F32
+            got_ref[...], other_ref[lanes], NT, preferred_element_type=F32
         )
         put(lanes, (cross - stats_ref[0:1, lanes] * mean) * stats_ref[1:2, lanes] * scale)
 
 
-def own_product(window_start, keep, got, stats, near, far, count):
+def own_product(window_start, keep, got, stats, doses, count):
     side = jax.ShapeDtypeStruct((ROWS, HALF), BF16)
 
     def kernel(start_ref, keep_ref, got_ref, stats_ref, *refs):
-        doses, (mine_ref, theirs_ref, wide) = (refs[0:2], refs[2:4]), refs[4:]
+        doses, (mine_ref, theirs_ref, wide) = refs[:2], refs[2:]
         core = lax.axis_index("samples")
 
         def put(lanes, values):
             wide[:, lanes] = values
 
-        correlations(count, keep_ref, got_ref, stats_ref, doses, put)
+        correlations(count, keep_ref, got_ref, stats_ref, doses, W, put)
         wide[:, W : W + SPILL] = jnp.zeros((ROWS, SPILL), F32)
         for ref, side in ((theirs_ref, 1 - core), (mine_ref, core)):
             last = []
@@ -271,21 +286,23 @@
     return pl.pallas_call(
         kernel,
         out_shape=(side, side),
-        in_specs=[SMEM] + [VMEM] * 7,
+        in_specs=[SMEM] + [VMEM] * 5,
         out_specs=(VMEM, VMEM),
         scratch_shapes=[pltpu.VMEM((ROWS, W + SPILL), F32)],
         compiler_params=params(16),
         cost_estimate=cost(1_500_000_000, 12_000_000),
         name="own_product",
-    )(window_start, keep, got, stats, *near, *far)
-
-
-def spill_product(keep, got, stats, near, count):
+    )(window_start, keep, got, stats, *doses)
+
+
+def spill_product(keep, got, stats, doses, count):
     def kernel(keep_ref, got_ref, stats_ref, dose_ref, other_ref, out_ref):
         def put(lanes, values):
             out_ref[:, lanes] = values.astype(BF16)
 
-        correlations(count, keep_ref, got_ref, stats_ref, ((dose_ref, other_ref),), put)
+        correlations(
+            count, keep_ref, got_ref, stats_ref, (dose_ref, other_ref), SPILL, put
+        )
 
     return pl.pallas_call(
         kernel,
@@ -295,10 +312,10 @@
         compiler_params=params(16),
         cost_estimate=cost(700_000_000, 6_000_000),
         name="spill_product",
-    )(keep, got, stats, *near)
-
-
-def merge_kernel(start_ref, mine_ref, other_ref, back0, back1, out_ref, wide, rows48):
+    )(keep, got, stats, *doses)
+
+
+def merge_kernel(start_ref, mine_ref, other_ref, back0, back1, out_hbm, wide, rows48, out_ref, sems):
     core = lax.axis_index("samples")
     back = (back0, back1)
     for c in range(2):
@@ -319,11 +336,22 @@
                 value = jnp.where(lane >= edge, wide[c, rows, window], own)
                 for t in range(HALF // LANES):
                     rows48[t, to, :] = value[:, t * LANES : (t + 1) * LANES]
-    for p in range(SLOTS + 1):
-        row = SLOTS if p == 0 else p - 1
-        for t in range(HALF // LANES):
-            genes = rows48[t, pl.ds(row, GENE_DEV, stride=48), :]
-            out_ref[p, :, t * LANES : (t + 1) * LANES] = genes.astype(BF16)
+    copies = []
+    for k, first in enumerate(range(0, SLOTS + 1, PIECE)):
+        end = min(first + PIECE, SLOTS + 1)
+        for p in range(first, end):
+            row = SLOTS if p == 0 else p - 1
+            for t in range(HALF // LANES):
+                genes = rows48[t, pl.ds(row, GENE_DEV, stride=48), :]
+                out_ref[p, :, t * LANES : (t + 1) * LANES] = genes.astype(BF16)
+        part = pl.ds(first, end - first)
+        copies.append(pltpu.make_async_copy(out_ref.at[part], out_hbm.at[part], sems.at[k]))
+        copies[-1].start()
+    for copy in copies:
+        copy.wait()
+
+
+PIECE = 11
 
 
 def merge(window_start, mine, other, back):
@@ -331,10 +359,12 @@
         merge_kernel,
         out_shape=jax.ShapeDtypeStruct((SLOTS + 1, GENE_DEV, HALF), BF16),
         in_specs=[SMEM] + [VMEM] * 4,
-        out_specs=VMEM,
+        out_specs=HBM,
         scratch_shapes=[
             pltpu.VMEM((2, ROWS, 2 * SPILL), F32),
             pltpu.VMEM((HALF // LANES, 48 * GENE_DEV, LANES), F32),
+            pltpu.VMEM((SLOTS + 1, GENE_DEV, HALF), BF16),
+            pltpu.SemaphoreType.DMA((pl.cdiv(SLOTS + 1, PIECE),)),
         ],
         compiler_params=params(24),
         cost_estimate=cost(2_000_000, 3_500_000),
@@ -359,23 +389,21 @@
 
     other_dose = exchanged(dosage)
     blocks = gather_blocks(gene_block, intron_counts, owners)
-    prev_expression = lax.ppermute(expression, "genes", onward)
     recv = lax.all_to_all(blocks, "genes", 0, 0, tiled=True)
-
-    stats = dose_stats(dosage, other_dose, count)
-    doses = (dosage, other_dose)
-
-    keep, give, *near = make_panel(recv, prev_expression, sizes, valid, doses, 1, 44)
+    tables = make_tables(expression, sizes, valid)
+    *doses, stats = dose_stats(dosage, other_dose, count)
+
+    keep, give = make_panel(recv, tables)
     got = exchanged(give)
-    piece = spill_product(keep, got, stats, near, count)
+    passed_keep = lax.ppermute(keep, "genes", onward)
+    passed_got = lax.ppermute(got, "genes", onward)
+    mine, theirs = own_product(window_start, keep, got, stats, doses, count)
+    other = exchanged(theirs)
+
+    piece = spill_product(passed_keep, passed_got, stats, doses, count)
     back = []
     for c in range(cores):
         back.append(lax.ppermute(piece, ("genes", "samples"), home[c]))
-
-    keep, give, *far = make_panel(recv, expression, sizes, valid, doses, 0, 40)
-    got = exchanged(give)
-    mine, theirs = own_product(window_start, keep, got, stats, near, far, count)
-    other = exchanged(theirs)
     out = merge(window_start, mine, other, back)
     return jnp.transpose(out, (1, 0, 2))
 

time: 109 us -> 90 us (0.83)
  blocking collectives: 58.2 us -> 0 us
  starting transfers between devices: 11.6 us -> 35.6 us
  waiting for transfers between devices: 12.5 us -> 33.8 us
  Pallas kernels: 22.9 us -> 17.2 us
    all_to_all x1 -> x0, blocking collectives: 58.2 us -> none  [shards(): recv = lax.all_to_all(blocks, 'genes', 0, 0, tiled=True)]
    all_to_all x0 -> x1, starting transfers between devices: none -> 24.1 us  [shards(): recv = lax.all_to_all(blocks, 'genes', 0, 0, tiled=True)]
    all_to_all x0 -> x1, waiting for transfers between devices: none -> 17.8 us  [shards(): recv = lax.all_to_all(blocks, 'genes', 0, 0, tiled=True)]
    pallas_call x4, Pallas kernels: 15.6 us -> 9.99 us  [the longest x1 4.66 us: dose_stats(): pl.pallas_call(functools.partial(dose_kernel, count), out_shape=(same, sa...]
    ppermute x1 -> x2, waiting for transfers between devices: 3.44 us -> 6.99 us  [the longest x1 6.99 us: shards(): passed_got = lax.ppermute(got, 'genes', onward)]
    ppermute x4 -> x3, starting transfers between devices: 5.2 us -> 2.98 us  [exchanged(): return lax.ppermute(x, 'samples', swap)]
    ppermute x1 -> x2, starting transfers between devices: 3.16 us -> 5.23 us  [the longest x1 2.91 us: shards(): passed_got = lax.ppermute(got, 'genes', onward)]
    unnamed x12 -> x8, local copies, waits for them, and re-layouts: 2.21 us -> 2.32 us
  transfers between devices with their start and end apart: 7 -> 8, of which waited for: 3 -> 4; matrix products, arithmetic and copies ran while one was open for 0% -> 0% of each run, Pallas kernels for 17% -> 17%
where the time goes in v3:
time: 90 us; the launch traced here: 89.1 us
  starting transfers between devices  35.6 us (40%)
  waiting for transfers between devices  33.8 us (38%)
  Pallas kernels  17.2 us (19%)
  local copies, waits for them, and re-layouts  2.32 us (3%)
    all_to_all x1, starting transfers between devices, shards(): recv = lax.all_to_all(blocks, 'genes', 0, 0, tiled=True)  24.1 us
    all_to_all x1, waiting for transfers between devices, shards(): recv = lax.all_to_all(blocks, 'genes', 0, 0, tiled=True)  17.8 us
    ppermute x2, waiting for transfers between devices, shards(): back.append(lax.ppermute(piece, ('genes', 'samples'), home[c]))  9 us
    ppermute x1, waiting for transfers between devices, shards(): passed_got = lax.ppermute(got, 'genes', onward)  6.99 us
    pallas_call x1, Pallas kernels, dose_stats(): pl.pallas_call(functools.partial(dose_kernel, count), out_shape=(same, sa...  4.66 us
    pallas_call x1, Pallas kernels, gather_blocks(): pl.pallas_call(gather_kernel, out_shape=jax.ShapeDtypeStruct((owners, 40,...  4.18 us
    pallas_call x1, Pallas kernels, own_product(): pl.pallas_call(kernel, out_shape=(side, side), in_specs=[SMEM] + [VMEM] *...  3.68 us
    ppermute x2, starting transfers between devices, shards(): back.append(lax.ppermute(piece, ('genes', 'samples'), home[c]))  3.26 us
  transfers between devices with their start and end apart: 8, of which 4 were waited for; matrix products, arithmetic and copies ran while one was open for 0% of the time, Pallas kernels for 17%

profile of v3, /device:TPU:515, one launch (start us, length us, event | category | flops | bytes accessed | tf_op | source)
XLA Modules:
  0.0 89.1 jit_solution(8855891760420665836)
XLA Ops:
  0.0 0.6 collective-permute-start.1
  0.6 4.2 %gather_blocks.1 = bf16[64,40,128]{2,1,0:T(8,128)(2,1)} custom-call(s32[512]{0:T(512)} %block_hbm.1, bf16[16,20480]{1,0:T(8,128)(2,1)} %counts_hbm.1), custom_call_target="tpu_custom_call" | custom-call | flops 10000000 | bytes 1 | tf_op jit(solution)/shard_map/gather_blocks/pallas_call | solution.py:74
  4.8 24.1 %all-to-all-start = ((bf16[64,40,128]{2,1,0:T(8,128)(2,1)}), bf16[64,40,128]{2,1,0:T(8,128)(2,1)S(1)}, u32[]{:S(2)}, u32[]{:S(2)}) async-start(bf16[64,40,128]{2,1,0:T(8,128)(2,1)} %gather_blocks.1), calls=%async_computation | async-start | bytes 1310720 | tf_op jit(solution)/shard_map/all_to_all | solution.py:392
  28.9 0.0 copy-start
  28.9 0.9 copy-done
  29.8 0.0 copy-start.1
  29.8 0.7 copy-done.1
  30.5 0.0 copy-start.2
  30.5 0.7 copy-done.2
  31.2 0.4 make_tables.1
  31.6 17.8 %all-to-all-done.recv_ref = bf16[64,40,128]{2,1,0:T(8,128)(2,1)S(1)} async-done(((bf16[64,40,128]{2,1,0:T(8,128)(2,1)}), bf16[64,40,128]{2,1,0:T(8,128)(2,1)S(1)}, u32[]{:S(2)}, u32[]{:S(2)}) %all-to-all-start) | async-done | bytes 655392 | tf_op jit(solution)/shard_map/all_to_all | solution.py:392
  49.4 0.8 make_panel.1
  50.2 1.8 %collective-permute-start = (bf16[168,1024]{1,0:T(8,128)(2,1)S(1)}, bf16[168,1024]{1,0:T(8,128)(2,1)S(1)}, u32[]{:S(2)}, u32[]{:S(2)}) collective-permute-start(bf16[168,1024]{1,0:T(8,128)(2,1)S(1)} %get-tuple-element.19), channel_id=1, source_target_pairs={{0,1},{1,0},{2,3},{3,2},{4,5},{5,4},{6,7},{7,6},{8,9},{9,8},{10,11... | collective-permute-start | bytes 1032200 | tf_op jit(solution)/shard_map/ppermute | solution.py:388
  52.0 0.0 copy-start.3
  52.0 2.3 %collective-permute-start.3 = (bf16[168,1024]{1,0:T(8,128)(2,1)S(1)}, bf16[168,1024]{1,0:T(8,128)(2,1)S(1)}, u32[]{:S(2)}, u32[]{:S(2)}) collective-permute-start(bf16[168,1024]{1,0:T(8,128)(2,1)S(1)} %get-tuple-element.18.keep_ref), channel_id=1, source_target_pairs={{0,2},{2,4},{4,6},{6,8},{8,10},{10,12},{12,14},{14,16},{16,18},{18... | collective-permute-start | bytes 1032200 | tf_op jit(solution)/shard_map/ppermute | solution.py:398
  54.3 0.0 collective-permute-done.got_ref
  54.3 2.9 %collective-permute-start.4 = (bf16[168,1024]{1,0:T(8,128)(2,1)S(1)}, bf16[168,1024]{1,0:T(8,128)(2,1)S(1)}, u32[]{:S(2)}, u32[]{:S(2)}) collective-permute-start(bf16[168,1024]{1,0:T(8,128)(2,1)S(1)} %collective-permute-done.got_ref), channel_id=1, source_target_pairs={{0,2},{2,4},{4,6},{6,8},{8,10},{10,12},{12,14},{14,16},{16,18},{18... | collective-permute-start | bytes 1032200 | tf_op jit(solution)/shard_map/ppermute | solution.py:399
  57.2 0.0 collective-permute-done.1.other_hbm
  57.3 4.7 %dose_stats.1 = (bf16[2048,1024]{1,0:T(8,128)(2,1)S(1)}, bf16[2048,1024]{1,0:T(8,128)(2,1)S(1)}, f32[8,2048]{1,0:T(8,128)S(1)}) custom-call(bf16[2048,1024]{1,0:T(8,128)(2,1)} %dose_hbm.1, bf16[2048,1024]{1,0:T(8,128)(2,1)} %collective-permute-done.1.other_hbm), custom_call_target="tpu_custom_call" | custom-call | flops 20000000 | bytes 16000000 | tf_op jit(solution)/shard_map/dose_stats/pallas_call | solution.py:237
  61.9 0.0 copy-done.3
  61.9 3.7 %own_product.1 = (bf16[168,1024]{1,0:T(8,128)(2,1)S(1)}, bf16[168,1024]{1,0:T(8,128)(2,1)S(1)}) custom-call(s32[8]{0:T(128)S(1)} %copy-done.3, bf16[168,1024]{1,0:T(8,128)(2,1)S(1)} %get-tuple-element.18.keep_ref, bf16[168,1024]{1,0:T(8,128)(2,1)S(1)} %collective-permute-done.got_ref, f32[8,2048]{1,0:T(8,128)S(1)} %get-tuple-element.20.stats_ref, ...), custom_call_target="tpu_custom_call" | custom-call | flops 1500000000 | bytes 12000000 | tf_op jit(solution)/shard_map/own_product/pallas_call | solution.py:286
  65.6 0.6 collective-permute-start.2
  66.2 0.0 collective-permute-done.3.keep_ref
  66.2 7.0 %collective-permute-done.4.got_ref = bf16[168,1024]{1,0:T(8,128)(2,1)S(1)} collective-permute-done((bf16[168,1024]{1,0:T(8,128)(2,1)S(1)}, bf16[168,1024]{1,0:T(8,128)(2,1)S(1)}, u32[]{:S(2)}, u32[]{:S(2)}) %collective-permute-start.4) | collective-permute-done | bytes 344096 | tf_op jit(solution)/shard_map/ppermute | solution.py:399
  73.2 1.6 %spill_product.1 = bf16[168,1024]{1,0:T(8,128)(2,1)S(1)} custom-call(bf16[168,1024]{1,0:T(8,128)(2,1)S(1)} %collective-permute-done.3.keep_ref, bf16[168,1024]{1,0:T(8,128)(2,1)S(1)} %collective-permute-done.4.got_ref, f32[8,2048]{1,0:T(8,128)S(1)} %get-tuple-element.20.stats_ref, bf16[2048,1024]{1,0:T(8,128)(2,1)S(1)} %get-tuple-element.21.refs_0_.dose_ref, ...), custom_call_target="tpu_custom_call" | custom-call | flops 700000000 | bytes 6000000 | tf_op jit(solution)/shard_map/spill_product/pallas_call | solution.py:307
  74.8 1.3 %collective-permute-start.5 = (bf16[168,1024]{1,0:T(8,128)(2,1)S(1)}, bf16[168,1024]{1,0:T(8,128)(2,1)S(1)}, u32[]{:S(2)}, u32[]{:S(2)}) collective-permute-start(bf16[168,1024]{1,0:T(8,128)(2,1)S(1)} %spill_product.1), channel_id=1, source_target_pairs={{2,1},{4,3},{6,5},{8,7},{10,9},{12,11},{14,13},{16,15},{18,17},{20... | collective-permute-start | bytes 1032200 | tf_op jit(solution)/shard_map/ppermute | solution.py:406
  76.1 2.0 %collective-permute-start.6 = (bf16[168,1024]{1,0:T(8,128)(2,1)S(1)}, bf16[168,1024]{1,0:T(8,128)(2,1)S(1)}, u32[]{:S(2)}, u32[]{:S(2)}) collective-permute-start(bf16[168,1024]{1,0:T(8,128)(2,1)S(1)} %spill_product.1), channel_id=1, source_target_pairs={{3,1},{5,3},{7,5},{9,7},{11,9},{13,11},{15,13},{17,15},{19,17},{21... | collective-permute-start | bytes 1032200 | tf_op jit(solution)/shard_map/ppermute | solution.py:406
  78.1 0.0 collective-permute-done.2.other_ref
  78.1 8.3 %collective-permute-done.5.back0 = bf16[168,1024]{1,0:T(8,128)(2,1)S(1)} collective-permute-done((bf16[168,1024]{1,0:T(8,128)(2,1)S(1)}, bf16[168,1024]{1,0:T(8,128)(2,1)S(1)}, u32[]{:S(2)}, u32[]{:S(2)}) %collective-permute-start.5) | collective-permute-done | bytes 344096 | tf_op jit(solution)/shard_map/ppermute | solution.py:406
  86.4 0.7 collective-permute-done.6.back1
  87.1 2.0 %merge_windows.1 = bf16[41,8,1024]{2,1,0:T(8,128)(2,1)} custom-call(s32[8]{0:T(128)S(1)} %copy-done.3, bf16[168,1024]{1,0:T(8,128)(2,1)S(1)} %get-tuple-element.23.mine_ref, bf16[168,1024]{1,0:T(8,128)(2,1)S(1)} %collective-permute-done.2.other_ref, bf16[168,1024]{1,0:T(8,128)(2,1)S(1)} %collective-permute-done.5.back0, ...), custom_call_target="tpu_custom_call" | custom-call | flops 2000000 | bytes 3500000 | tf_op jit(solution)/shard_map/merge_windows/pallas_call | solution.py:358
Async XLA Ops:
  0.0 57.2 %collective-permute-start.1 = (bf16[2048,1024]{1,0:T(8,128)(2,1)}, bf16[2048,1024]{1,0:T(8,128)(2,1)}, u32[]{:S(2)}, u32[]{:S(2)}) collective-permute-start(bf16[2048,1024]{1,0:T(8,128)(2,1)} %dose_hbm.1), channel_id=1, source_target_pairs={{0,1},{1,0},{2,3},{3,2},{4,5},{5,4},{6,7},{7,6},{8,9},{9,8},{10,11... | collective-permute-start | bytes 12582920 | tf_op jit(solution)/shard_map/ppermute | solution.py:388
  4.8 44.6 %all-to-all-start = ((bf16[64,40,128]{2,1,0:T(8,128)(2,1)}), bf16[64,40,128]{2,1,0:T(8,128)(2,1)S(1)}, u32[]{:S(2)}, u32[]{:S(2)}) async-start(bf16[64,40,128]{2,1,0:T(8,128)(2,1)} %gather_blocks.1), calls=%async_computation | async-start | bytes 1310720 | tf_op jit(solution)/shard_map/all_to_all | solution.py:392
  28.9 0.9 copy-start
  29.8 0.7 copy-start.1
  30.5 0.7 copy-start.2
  50.2 4.1 %collective-permute-start = (bf16[168,1024]{1,0:T(8,128)(2,1)S(1)}, bf16[168,1024]{1,0:T(8,128)(2,1)S(1)}, u32[]{:S(2)}, u32[]{:S(2)}) collective-permute-start(bf16[168,1024]{1,0:T(8,128)(2,1)S(1)} %get-tuple-element.19), channel_id=1, source_target_pairs={{0,1},{1,0},{2,3},{3,2},{4,5},{5,4},{6,7},{7,6},{8,9},{9,8},{10,11... | collective-permute-start | bytes 1032200 | tf_op jit(solution)/shard_map/ppermute | solution.py:388
  52.0 9.9 %copy-start.3 = (s32[8]{0:T(128)S(1)}, s32[8]{0:T(128)}, u32[]{:S(2)}) copy-start(s32[8]{0:T(128)} %start_ref.3) | copy-start | bytes 100
  52.0 14.2 %collective-permute-start.3 = (bf16[168,1024]{1,0:T(8,128)(2,1)S(1)}, bf16[168,1024]{1,0:T(8,128)(2,1)S(1)}, u32[]{:S(2)}, u32[]{:S(2)}) collective-permute-start(bf16[168,1024]{1,0:T(8,128)(2,1)S(1)} %get-tuple-element.18.keep_ref), channel_id=1, source_target_pairs={{0,2},{2,4},{4,6},{6,8},{8,10},{10,12},{12,14},{14,16},{16,18},{18... | collective-permute-start | bytes 1032200 | tf_op jit(solution)/shard_map/ppermute | solution.py:398
  54.3 18.9 %collective-permute-start.4 = (bf16[168,1024]{1,0:T(8,128)(2,1)S(1)}, bf16[168,1024]{1,0:T(8,128)(2,1)S(1)}, u32[]{:S(2)}, u32[]{:S(2)}) collective-permute-start(bf16[168,1024]{1,0:T(8,128)(2,1)S(1)} %collective-permute-done.got_ref), channel_id=1, source_target_pairs={{0,2},{2,4},{4,6},{6,8},{8,10},{10,12},{12,14},{14,16},{16,18},{18... | collective-permute-start | bytes 1032200 | tf_op jit(solution)/shard_map/ppermute | solution.py:399
  65.6 12.5 %collective-permute-start.2 = (bf16[168,1024]{1,0:T(8,128)(2,1)S(1)}, bf16[168,1024]{1,0:T(8,128)(2,1)S(1)}, u32[]{:S(2)}, u32[]{:S(2)}) collective-permute-start(bf16[168,1024]{1,0:T(8,128)(2,1)S(1)} %get-tuple-element.24), channel_id=1, source_target_pairs={{0,1},{1,0},{2,3},{3,2},{4,5},{5,4},{6,7},{7,6},{8,9},{9,8},{10,11... | collective-permute-start | bytes 1032200 | tf_op jit(solution)/shard_map/ppermute | solution.py:388
  74.8 11.5 %collective-permute-start.5 = (bf16[168,1024]{1,0:T(8,128)(2,1)S(1)}, bf16[168,1024]{1,0:T(8,128)(2,1)S(1)}, u32[]{:S(2)}, u32[]{:S(2)}) collective-permute-start(bf16[168,1024]{1,0:T(8,128)(2,1)S(1)} %spill_product.1), channel_id=1, source_target_pairs={{2,1},{4,3},{6,5},{8,7},{10,9},{12,11},{14,13},{16,15},{18,17},{20... | collective-permute-start | bytes 1032200 | tf_op jit(solution)/shard_map/ppermute | solution.py:406
  76.1 11.0 %collective-permute-start.6 = (bf16[168,1024]{1,0:T(8,128)(2,1)S(1)}, bf16[168,1024]{1,0:T(8,128)(2,1)S(1)}, u32[]{:S(2)}, u32[]{:S(2)}) collective-permute-start(bf16[168,1024]{1,0:T(8,128)(2,1)S(1)} %spill_product.1), channel_id=1, source_target_pairs={{3,1},{5,3},{7,5},{9,7},{11,9},{13,11},{15,13},{17,15},{19,17},{21... | collective-permute-start | bytes 1032200 | tf_op jit(solution)/shard_map/ppermute | solution.py:406

commit v4 on v3

--- a/solution.py
+++ b/solution.py
@@ -246,12 +246,12 @@
     )(dosage, other)
 
 
-def correlations(count, keep_ref, got_ref, stats_ref, doses, variants, put):
+def correlations(count, keep_ref, got_ref, stats_ref, doses, put):
     sy, syy = row_sums((keep_ref, got_ref))
     mean = sy / count
     scale = lax.rsqrt(jnp.maximum(syy - sy * mean, 1.0))
     dose_ref, other_ref = doses
-    for i in range(variants // BLOCK):
+    for i in range(W // BLOCK):
         lanes = slice(i * BLOCK, (i + 1) * BLOCK)
         cross = lax.dot_general(keep_ref[...], dose_ref[lanes], NT, preferred_element_type=F32)
         cross = cross + lax.dot_general(
@@ -270,7 +270,7 @@
         def put(lanes, values):
             wide[:, lanes] = values
 
-        correlations(count, keep_ref, got_ref, stats_ref, doses, W, put)
+        correlations(count, keep_ref, got_ref, stats_ref, doses, put)
         wide[:, W : W + SPILL] = jnp.zeros((ROWS, SPILL), F32)
         for ref, side in ((theirs_ref, 1 - core), (mine_ref, core)):
             last = []
@@ -295,24 +295,52 @@
     )(window_start, keep, got, stats, *doses)
 
 
-def spill_product(keep, got, stats, doses, count):
-    def kernel(keep_ref, got_ref, stats_ref, dose_ref, other_ref, out_ref):
-        def put(lanes, values):
-            out_ref[:, lanes] = values.astype(BF16)
-
-        correlations(
-            count, keep_ref, got_ref, stats_ref, (dose_ref, other_ref), SPILL, put
-        )
+def spill_first(keep, dose):
+    def kernel(keep_ref, dose_ref, out_ref):
+        for i in range(SPILL // BLOCK):
+            lanes = slice(i * BLOCK, (i + 1) * BLOCK)
+            out_ref[:, lanes] = lax.dot_general(
+                keep_ref[...], dose_ref[lanes], NT, preferred_element_type=F32
+            )
+        sy, syy = row_sums((keep_ref,))
+        lane = lax.broadcasted_iota(jnp.int32, (ROWS, LANES), 1)
+        out_ref[:, SPILL : SPILL + LANES] = jnp.where(lane == 0, sy, syy)
+
+    return pl.pallas_call(
+        kernel,
+        out_shape=jax.ShapeDtypeStruct((ROWS, SPILL + LANES), F32),
+        in_specs=[VMEM] * 2,
+        out_specs=VMEM,
+        compiler_params=params(16),
+        cost_estimate=cost(350_000_000, 3_000_000),
+        name="spill_first",
+    )(keep, dose)
+
+
+def spill_product(part, got, stats, other, count):
+    def kernel(part_ref, got_ref, stats_ref, other_ref, out_ref):
+        sy, syy = row_sums((got_ref,))
+        sy = sy + part_ref[:, SPILL : SPILL + 1]
+        syy = syy + part_ref[:, SPILL + 1 : SPILL + 2]
+        mean = sy / count
+        scale = lax.rsqrt(jnp.maximum(syy - sy * mean, 1.0))
+        for i in range(SPILL // BLOCK):
+            lanes = slice(i * BLOCK, (i + 1) * BLOCK)
+            cross = part_ref[:, lanes] + lax.dot_general(
+                got_ref[...], other_ref[lanes], NT, preferred_element_type=F32
+            )
+            value = (cross - stats_ref[0:1, lanes] * mean) * stats_ref[1:2, lanes] * scale
+            out_ref[:, lanes] = value.astype(BF16)
 
     return pl.pallas_call(
         kernel,
         out_shape=jax.ShapeDtypeStruct((ROWS, SPILL), BF16),
-        in_specs=[VMEM] * 5,
+        in_specs=[VMEM] * 4,
         out_specs=VMEM,
         compiler_params=params(16),
-        cost_estimate=cost(700_000_000, 6_000_000),
+        cost_estimate=cost(350_000_000, 3_000_000),
         name="spill_product",
-    )(keep, got, stats, *doses)
+    )(part, got, stats, other)
 
 
 def merge_kernel(start_ref, mine_ref, other_ref, back0, back1, out_hbm, wide, rows48, out_ref, sems):
@@ -400,7 +428,8 @@
     mine, theirs = own_product(window_start, keep, got, stats, doses, count)
     other = exchanged(theirs)
 
-    piece = spill_product(passed_keep, passed_got, stats, doses, count)
+    part = spill_first(passed_keep, doses[0])
+    piece = spill_product(part, passed_got, stats, doses[1], count)
     back = []
     for c in range(cores):
         back.append(lax.ppermute(piece, ("genes", "samples"), home[c]))

time: 90 us -> 89.3 us (level)
  no operation moved by 1% of the time
where the time goes in v4:
time: 89.3 us; the launch traced here: 88.4 us
  starting transfers between devices  35.6 us (40%)
  waiting for transfers between devices  33 us (37%)
  Pallas kernels  17.4 us (19%)
  local copies, waits for them, and re-layouts  2.32 us (3%)
    all_to_all x1, starting transfers between devices, shards(): recv = lax.all_to_all(blocks, 'genes', 0, 0, tiled=True)  24.1 us
    all_to_all x1, waiting for transfers between devices, shards(): recv = lax.all_to_all(blocks, 'genes', 0, 0, tiled=True)  17.8 us
    ppermute x2, waiting for transfers between devices, shards(): back.append(lax.ppermute(piece, ('genes', 'samples'), home[c]))  9 us
    ppermute x1, waiting for transfers between devices, shards(): passed_got = lax.ppermute(got, 'genes', onward)  6.13 us
    pallas_call x1, Pallas kernels, dose_stats(): pl.pallas_call(functools.partial(dose_kernel, count), out_shape=(same, sa...  4.66 us
    pallas_call x1, Pallas kernels, gather_blocks(): pl.pallas_call(gather_kernel, out_shape=jax.ShapeDtypeStruct((owners, 40,...  4.18 us
    pallas_call x1, Pallas kernels, own_product(): pl.pallas_call(kernel, out_shape=(side, side), in_specs=[SMEM] + [VMEM] *...  3.68 us
    ppermute x2, starting transfers between devices, shards(): back.append(lax.ppermute(piece, ('genes', 'samples'), home[c]))  3.26 us
  transfers between devices with their start and end apart: 8, of which 4 were waited for; matrix products, arithmetic and copies ran while one was open for 0% of the time, Pallas kernels for 17%

profile of v4, /device:TPU:515, one launch (start us, length us, event | category | flops | bytes accessed | tf_op | source)
XLA Modules:
  0.0 88.4 jit_solution(7568937201165231029)
XLA Ops:
  0.0 0.6 collective-permute-start.1
  0.6 4.2 %gather_blocks.1 = bf16[64,40,128]{2,1,0:T(8,128)(2,1)} custom-call(s32[512]{0:T(512)} %block_hbm.1, bf16[16,20480]{1,0:T(8,128)(2,1)} %counts_hbm.1), custom_call_target="tpu_custom_call" | custom-call | flops 10000000 | bytes 1 | tf_op jit(solution)/shard_map/gather_blocks/pallas_call | solution.py:74
  4.8 24.1 %all-to-all-start = ((bf16[64,40,128]{2,1,0:T(8,128)(2,1)}), bf16[64,40,128]{2,1,0:T(8,128)(2,1)S(1)}, u32[]{:S(2)}, u32[]{:S(2)}) async-start(bf16[64,40,128]{2,1,0:T(8,128)(2,1)} %gather_blocks.1), calls=%async_computation | async-start | bytes 1310720 | tf_op jit(solution)/shard_map/all_to_all | solution.py:420
  28.9 0.0 copy-start
  28.9 0.9 copy-done
  29.8 0.0 copy-start.1
  29.8 0.7 copy-done.1
  30.5 0.0 copy-start.2
  30.5 0.7 copy-done.2
  31.2 0.4 make_tables.1
  31.6 17.8 %all-to-all-done.recv_ref = bf16[64,40,128]{2,1,0:T(8,128)(2,1)S(1)} async-done(((bf16[64,40,128]{2,1,0:T(8,128)(2,1)}), bf16[64,40,128]{2,1,0:T(8,128)(2,1)S(1)}, u32[]{:S(2)}, u32[]{:S(2)}) %all-to-all-start) | async-done | bytes 655392 | tf_op jit(solution)/shard_map/all_to_all | solution.py:420
  49.4 0.8 make_panel.1
  50.2 1.8 %collective-permute-start = (bf16[168,1024]{1,0:T(8,128)(2,1)S(1)}, bf16[168,1024]{1,0:T(8,128)(2,1)S(1)}, u32[]{:S(2)}, u32[]{:S(2)}) collective-permute-start(bf16[168,1024]{1,0:T(8,128)(2,1)S(1)} %get-tuple-element.19), channel_id=1, source_target_pairs={{0,1},{1,0},{2,3},{3,2},{4,5},{5,4},{6,7},{7,6},{8,9},{9,8},{10,11... | collective-permute-start | bytes 1032200 | tf_op jit(solution)/shard_map/ppermute | solution.py:416
  52.0 0.0 copy-start.3
  52.0 2.3 %collective-permute-start.3 = (bf16[168,1024]{1,0:T(8,128)(2,1)S(1)}, bf16[168,1024]{1,0:T(8,128)(2,1)S(1)}, u32[]{:S(2)}, u32[]{:S(2)}) collective-permute-start(bf16[168,1024]{1,0:T(8,128)(2,1)S(1)} %get-tuple-element.18.keep_ref), channel_id=1, source_target_pairs={{0,2},{2,4},{4,6},{6,8},{8,10},{10,12},{12,14},{14,16},{16,18},{18... | collective-permute-start | bytes 1032200 | tf_op jit(solution)/shard_map/ppermute | solution.py:426
  54.3 0.0 collective-permute-done.got_ref
  54.3 2.9 %collective-permute-start.4 = (bf16[168,1024]{1,0:T(8,128)(2,1)S(1)}, bf16[168,1024]{1,0:T(8,128)(2,1)S(1)}, u32[]{:S(2)}, u32[]{:S(2)}) collective-permute-start(bf16[168,1024]{1,0:T(8,128)(2,1)S(1)} %collective-permute-done.got_ref), channel_id=1, source_target_pairs={{0,2},{2,4},{4,6},{6,8},{8,10},{10,12},{12,14},{14,16},{16,18},{18... | collective-permute-start | bytes 1032200 | tf_op jit(solution)/shard_map/ppermute | solution.py:427
  57.2 0.0 collective-permute-done.1.other_hbm
  57.3 4.7 %dose_stats.1 = (bf16[2048,1024]{1,0:T(8,128)(2,1)S(1)}, bf16[2048,1024]{1,0:T(8,128)(2,1)S(1)}, f32[8,2048]{1,0:T(8,128)S(1)}) custom-call(bf16[2048,1024]{1,0:T(8,128)(2,1)} %dose_hbm.1, bf16[2048,1024]{1,0:T(8,128)(2,1)} %collective-permute-done.1.other_hbm), custom_call_target="tpu_custom_call" | custom-call | flops 20000000 | bytes 16000000 | tf_op jit(solution)/shard_map/dose_stats/pallas_call | solution.py:237
  61.9 0.0 copy-done.3
  61.9 3.7 %own_product.1 = (bf16[168,1024]{1,0:T(8,128)(2,1)S(1)}, bf16[168,1024]{1,0:T(8,128)(2,1)S(1)}) custom-call(s32[8]{0:T(128)S(1)} %copy-done.3, bf16[168,1024]{1,0:T(8,128)(2,1)S(1)} %get-tuple-element.18.keep_ref, bf16[168,1024]{1,0:T(8,128)(2,1)S(1)} %collective-permute-done.got_ref, f32[8,2048]{1,0:T(8,128)S(1)} %get-tuple-element.20.stats_ref, ...), custom_call_target="tpu_custom_call" | custom-call | flops 1500000000 | bytes 12000000 | tf_op jit(solution)/shard_map/own_product/pallas_call | solution.py:286
  65.6 0.6 collective-permute-start.2
  66.2 0.0 collective-permute-done.3.keep_ref
  66.2 0.9 spill_first.1.part_ref
  67.1 6.1 %collective-permute-done.4.got_ref = bf16[168,1024]{1,0:T(8,128)(2,1)S(1)} collective-permute-done((bf16[168,1024]{1,0:T(8,128)(2,1)S(1)}, bf16[168,1024]{1,0:T(8,128)(2,1)S(1)}, u32[]{:S(2)}, u32[]{:S(2)}) %collective-permute-start.4) | collective-permute-done | bytes 344096 | tf_op jit(solution)/shard_map/ppermute | solution.py:427
  73.2 0.9 %spill_product.1 = bf16[168,1024]{1,0:T(8,128)(2,1)S(1)} custom-call(f32[168,1152]{1,0:T(8,128)S(1)} %spill_first.1.part_ref, bf16[168,1024]{1,0:T(8,128)(2,1)S(1)} %collective-permute-done.4.got_ref, f32[8,2048]{1,0:T(8,128)S(1)} %get-tuple-element.20.stats_ref, bf16[2048,1024]{1,0:T(8,128)(2,1)S(1)} %get-tuple-element.22.refs_1_.other_ref), custom_call_target="tpu_custom_call" | custom-call | flops 350000000 | bytes 3000000 | tf_op jit(solution)/shard_map/spill_product/pallas_call | solution.py:335
  74.1 1.3 %collective-permute-start.5 = (bf16[168,1024]{1,0:T(8,128)(2,1)S(1)}, bf16[168,1024]{1,0:T(8,128)(2,1)S(1)}, u32[]{:S(2)}, u32[]{:S(2)}) collective-permute-start(bf16[168,1024]{1,0:T(8,128)(2,1)S(1)} %spill_product.1), channel_id=1, source_target_pairs={{2,1},{4,3},{6,5},{8,7},{10,9},{12,11},{14,13},{16,15},{18,17},{20... | collective-permute-start | bytes 1032200 | tf_op jit(solution)/shard_map/ppermute | solution.py:435
  75.4 2.0 %collective-permute-start.6 = (bf16[168,1024]{1,0:T(8,128)(2,1)S(1)}, bf16[168,1024]{1,0:T(8,128)(2,1)S(1)}, u32[]{:S(2)}, u32[]{:S(2)}) collective-permute-start(bf16[168,1024]{1,0:T(8,128)(2,1)S(1)} %spill_product.1), channel_id=1, source_target_pairs={{3,1},{5,3},{7,5},{9,7},{11,9},{13,11},{15,13},{17,15},{19,17},{21... | collective-permute-start | bytes 1032200 | tf_op jit(solution)/shard_map/ppermute | solution.py:435
  77.4 0.0 collective-permute-done.2.other_ref
  77.4 8.3 %collective-permute-done.5.back0 = bf16[168,1024]{1,0:T(8,128)(2,1)S(1)} collective-permute-done((bf16[168,1024]{1,0:T(8,128)(2,1)S(1)}, bf16[168,1024]{1,0:T(8,128)(2,1)S(1)}, u32[]{:S(2)}, u32[]{:S(2)}) %collective-permute-start.5) | collective-permute-done | bytes 344096 | tf_op jit(solution)/shard_map/ppermute | solution.py:435
  85.7 0.7 collective-permute-done.6.back1
  86.4 2.0 %merge_windows.1 = bf16[41,8,1024]{2,1,0:T(8,128)(2,1)} custom-call(s32[8]{0:T(128)S(1)} %copy-done.3, bf16[168,1024]{1,0:T(8,128)(2,1)S(1)} %get-tuple-element.23.mine_ref, bf16[168,1024]{1,0:T(8,128)(2,1)S(1)} %collective-permute-done.2.other_ref, bf16[168,1024]{1,0:T(8,128)(2,1)S(1)} %collective-permute-done.5.back0, ...), custom_call_target="tpu_custom_call" | custom-call | flops 2000000 | bytes 3500000 | tf_op jit(solution)/shard_map/merge_windows/pallas_call | solution.py:386
Async XLA Ops:
  0.0 57.2 %collective-permute-start.1 = (bf16[2048,1024]{1,0:T(8,128)(2,1)}, bf16[2048,1024]{1,0:T(8,128)(2,1)}, u32[]{:S(2)}, u32[]{:S(2)}) collective-permute-start(bf16[2048,1024]{1,0:T(8,128)(2,1)} %dose_hbm.1), channel_id=1, source_target_pairs={{0,1},{1,0},{2,3},{3,2},{4,5},{5,4},{6,7},{7,6},{8,9},{9,8},{10,11... | collective-permute-start | bytes 12582920 | tf_op jit(solution)/shard_map/ppermute | solution.py:416
  4.8 44.6 %all-to-all-start = ((bf16[64,40,128]{2,1,0:T(8,128)(2,1)}), bf16[64,40,128]{2,1,0:T(8,128)(2,1)S(1)}, u32[]{:S(2)}, u32[]{:S(2)}) async-start(bf16[64,40,128]{2,1,0:T(8,128)(2,1)} %gather_blocks.1), calls=%async_computation | async-start | bytes 1310720 | tf_op jit(solution)/shard_map/all_to_all | solution.py:420
  28.9 0.9 %copy-start = (s32[512,40]{0,1:T(8,128)S(1)}, s32[512,40]{0,1:T(8,128)}, u32[]{:S(2)}) copy-start(s32[512,40]{0,1:T(8,128)} %param.11) | copy-start | bytes 245764
  29.8 0.7 copy-start.1
  30.5 0.7 copy-start.2
  50.2 4.1 %collective-permute-start = (bf16[168,1024]{1,0:T(8,128)(2,1)S(1)}, bf16[168,1024]{1,0:T(8,128)(2,1)S(1)}, u32[]{:S(2)}, u32[]{:S(2)}) collective-permute-start(bf16[168,1024]{1,0:T(8,128)(2,1)S(1)} %get-tuple-element.19), channel_id=1, source_target_pairs={{0,1},{1,0},{2,3},{3,2},{4,5},{5,4},{6,7},{7,6},{8,9},{9,8},{10,11... | collective-permute-start | bytes 1032200 | tf_op jit(solution)/shard_map/ppermute | solution.py:416
  52.0 9.9 %copy-start.3 = (s32[8]{0:T(128)S(1)}, s32[8]{0:T(128)}, u32[]{:S(2)}) copy-start(s32[8]{0:T(128)} %start_ref.3) | copy-start | bytes 100
  52.0 14.2 %collective-permute-start.3 = (bf16[168,1024]{1,0:T(8,128)(2,1)S(1)}, bf16[168,1024]{1,0:T(8,128)(2,1)S(1)}, u32[]{:S(2)}, u32[]{:S(2)}) collective-permute-start(bf16[168,1024]{1,0:T(8,128)(2,1)S(1)} %get-tuple-element.18.keep_ref), channel_id=1, source_target_pairs={{0,2},{2,4},{4,6},{6,8},{8,10},{10,12},{12,14},{14,16},{16,18},{18... | collective-permute-start | bytes 1032200 | tf_op jit(solution)/shard_map/ppermute | solution.py:426
  54.3 18.9 %collective-permute-start.4 = (bf16[168,1024]{1,0:T(8,128)(2,1)S(1)}, bf16[168,1024]{1,0:T(8,128)(2,1)S(1)}, u32[]{:S(2)}, u32[]{:S(2)}) collective-permute-start(bf16[168,1024]{1,0:T(8,128)(2,1)S(1)} %collective-permute-done.got_ref), channel_id=1, source_target_pairs={{0,2},{2,4},{4,6},{6,8},{8,10},{10,12},{12,14},{14,16},{16,18},{18... | collective-permute-start | bytes 1032200 | tf_op jit(solution)/shard_map/ppermute | solution.py:427
  65.6 11.8 %collective-permute-start.2 = (bf16[168,1024]{1,0:T(8,128)(2,1)S(1)}, bf16[168,1024]{1,0:T(8,128)(2,1)S(1)}, u32[]{:S(2)}, u32[]{:S(2)}) collective-permute-start(bf16[168,1024]{1,0:T(8,128)(2,1)S(1)} %get-tuple-element.24), channel_id=1, source_target_pairs={{0,1},{1,0},{2,3},{3,2},{4,5},{5,4},{6,7},{7,6},{8,9},{9,8},{10,11... | collective-permute-start | bytes 1032200 | tf_op jit(solution)/shard_map/ppermute | solution.py:416
  74.1 11.5 %collective-permute-start.5 = (bf16[168,1024]{1,0:T(8,128)(2,1)S(1)}, bf16[168,1024]{1,0:T(8,128)(2,1)S(1)}, u32[]{:S(2)}, u32[]{:S(2)}) collective-permute-start(bf16[168,1024]{1,0:T(8,128)(2,1)S(1)} %spill_product.1), channel_id=1, source_target_pairs={{2,1},{4,3},{6,5},{8,7},{10,9},{12,11},{14,13},{16,15},{18,17},{20... | collective-permute-start | bytes 1032200 | tf_op jit(solution)/shard_map/ppermute | solution.py:435
  75.4 11.0 %collective-permute-start.6 = (bf16[168,1024]{1,0:T(8,128)(2,1)S(1)}, bf16[168,1024]{1,0:T(8,128)(2,1)S(1)}, u32[]{:S(2)}, u32[]{:S(2)}) collective-permute-start(bf16[168,1024]{1,0:T(8,128)(2,1)S(1)} %spill_product.1), channel_id=1, source_target_pairs={{3,1},{5,3},{7,5},{9,7},{11,9},{13,11},{15,13},{17,15},{19,17},{21... | collective-permute-start | bytes 1032200 | tf_op jit(solution)/shard_map/ppermute | solution.py:435
